TPU v7x, 32 devices: a whole 2x2x4 slice. The times are simulated.
32 devices in a mesh: rows: 8 (over y, x, core), tp: 4 (over z).
Axes of the slice: x: 2, y: 2, z: 4, core: 2. Of those that a mesh axis runs over, the one named last changes fastest.
Arguments:
- train_up: bfloat16 [5120, 20480], P('rows', 'tp'), may hold values from -0.078125 to 0.078125
- low_up: bfloat16 [5120, 16], P('rows'), may hold values from -0.078125 to 0.078125
- high_up: bfloat16 [16, 20480], P(None, 'tp'), may hold values from -1.5 to 1.5
- norm_train: float32 [5120], P(('rows', 'tp')), may hold values from 0.25 to 1.75
- norm_step: float32 [5120], P(('rows', 'tp')), may hold values from -0.3 to 0.3
Outputs:
- ready_up: bfloat16 [20480, 5120], P('tp')
- serve_norm: bfloat16 [5120], replicated
All inputs are finite; a program needn't handle non-finite values.
Results may differ from a plain program's by a relative error of at most 0.001.
Values may be sent and summed in bfloat16 or wider, within the bound.
A program may use at most 192 MiB of HBM per device.

v0:
```python
import jax
import jax.numpy as jnp
from jax import lax
from jax.sharding import PartitionSpec as P

mix_rate = 2.0


def per_device(train_up, low_up, high_up, norm_train, norm_step):
    latest_up = train_up.astype(jnp.float32) + mix_rate * jnp.dot(
        low_up, high_up, preferred_element_type=jnp.float32
    )
    narrow_up = latest_up.astype(jnp.bfloat16)
    ready_up = lax.all_gather(narrow_up, "rows", axis=0, tiled=True)
    ready_up = ready_up.T
    serve_norm = lax.all_gather(
        (norm_train + norm_step).astype(jnp.bfloat16), ("rows", "tp"), axis=0, tiled=True
    )
    return (ready_up, serve_norm)


def solution(mesh):
    placed = (P("rows", "tp"), P("rows", None), P(None, "tp"), P(("rows", "tp")), P(("rows", "tp")))
    return jax.shard_map(
        per_device, mesh=mesh, in_specs=placed, out_specs=(P("tp", None), P()), check_vma=False
    )
```

profile of v0, /device:TPU:0, one launch (start us, length us, event | category | flops | bytes accessed | tf_op | source)
XLA Modules:
  0.0 336.6 jit_solution(3727503124252561573)
XLA Ops:
  7.2 0.0 copy-start
  7.2 0.0 copy-start.2
  7.2 0.0 copy-start.3
  7.2 0.0 all-gather.2.cloned.1.call-start
  7.2 0.8 copy-done
  8.1 7.6 %add_convert_fusion = bf16[640,5120]{1,0:T(8,128)(2,1)} fusion(bf16[640,5120]{1,0:T(8,128)(2,1)} %param.5, bf16[640,16]{0,1:T(8,128)(2,1)} %param.6, bf16[16,5120]{1,0:T(8,128)(2,1)S(1)} %copy-done), kind=kOutput, calls=%fused_computation | convolution fusion | flops 117964800 | bytes 13291520 | tf_op jit(solution)/shard_map/dot_general | solution.py:10
  15.7 0.0 all-gather.2.cloned.1.call-update
  15.7 0.0 copy-done.2
  15.7 0.0 copy-done.3
  15.7 0.2 dynamic-update-slice
  16.0 42.7 %all-reduce = bf16[5120]{0:T(1024)(128)(2,1)} all-reduce(bf16[5120]{0:T(1024)(128)(2,1)S(1)} %dynamic-update-slice), channel_id=1, replica_groups=mesh['rows'=8,'tp'=4] {'rows','tp'}, use_global_device_ids=true, to_apply=%add | all-reduce | flops 5120 | bytes 20480
  58.7 201.4 %all-gather.2.cloned.1.call-done = bf16[5120,5120]{1,0:T(8,128)(2,1)} async-done(((bf16[640,5120]{1,0:T(8,128)(2,1)}), bf16[5120,5120]{1,0:T(8,128)(2,1)}) %all-gather.2.cloned.1.call-update) | async-done | bytes 52428816 | tf_op jit(solution)/shard_map/all_gather | solution.py:14
  260.1 0.0 copy-start.1
  260.1 69.6 %copy.7 = bf16[5120,5120]{1,0:T(8,128)(2,1)} copy(bf16[5120,5120]{0,1:T(8,128)(2,1)} %bitcast.3) | data formatting | bytes 104857600
  329.7 0.0 copy-done.1
  (2 shorter events, 0.0 us)
Async XLA Ops:
  7.2 0.9 copy-start
  7.2 8.5 %copy-start.2 = (f32[160]{0:T(256)S(1)}, f32[160]{0:T(256)}, u32[]{:S(2)}) copy-start(f32[160]{0:T(256)} %param.8) | copy-start | bytes 1924
  7.2 8.5 %copy-start.3 = (f32[160]{0:T(256)S(1)}, f32[160]{0:T(256)}, u32[]{:S(2)}) copy-start(f32[160]{0:T(256)} %param.9) | copy-start | bytes 1924
  7.2 252.9 %all-gather.2.cloned.1.call-start = ((), (), s32[]{:S(2)}) async-start(), calls=%async_computation | async-start | bytes 58982400 | tf_op jit(solution)/shard_map/all_gather | solution.py:14
  260.1 69.6 %copy-start.1 = (bf16[16,5120]{1,0:T(8,128)(2,1)S(1)}, bf16[16,5120]{1,0:T(8,128)(2,1)}, u32[]{:S(2)}) copy-start(bf16[16,5120]{1,0:T(8,128)(2,1)} %param.7) | copy-start | bytes 491524
Sparse Core Ops, SparseCore 0:
  15.8 244.2 all-gather.1
where the time goes:
time: 339 us; the launch traced here: 337 us
  waiting for transfers between devices  201 us (59%)
  local copies, waits for them, and re-layouts  70.8 us (21%)
  blocking collectives  42.7 us (13%)
  between operations  14.1 us (4%)
  matrix products  7.56 us (2%)
    all_gather x1, waiting for transfers between devices, per_device(): ready_up = lax.all_gather(narrow_up, 'rows', axis=0, tiled=True)  201 us
    unnamed x11, local copies, waits for them, and re-layouts  70.8 us
    unnamed x1, blocking collectives  42.7 us
    dot_general x1, matrix products, per_device(): jnp.dot(low_up, high_up, preferred_element_type=jnp.float32)  7.56 us
  transfers between devices with their start and end apart: 1, of which 1 were waited for; matrix products, arithmetic and copies ran while one was open for 0% of the time, Pallas kernels for 0%

commit v1 on v0

v1 whole, which is shorter than its diff:
```python
import functools

import jax
import jax.numpy as jnp
from jax import lax
from jax.experimental import pallas as pl
from jax.experimental.pallas import tpu as pltpu
from jax.sharding import PartitionSpec as P


mix_rate = 2.0
PIECES = 8
ANY = pl.BlockSpec(memory_space=pl.ANY)


def merge_kernel(train_ref, low_ref, high_ref, norm_ref, *refs, tile):
    piece_ref = refs[-1]
    rows = train_ref.shape[1]
    for start in range(0, rows, tile):
        cols = slice(start, start + tile)
        update = lax.dot_general(
            high_ref[:, cols], low_ref[...], (((0,), (0,)), ((), ())), preferred_element_type=jnp.float32
        )
        latest = train_ref[:, cols].T.astype(jnp.float32) + mix_rate * update
        piece_ref[cols, :] = latest.astype(jnp.bfloat16)
    if piece_ref.shape[0] > rows:
        piece_ref[rows:, :] = jnp.broadcast_to(norm_ref[...], (piece_ref.shape[0] - rows, norm_ref.shape[1]))


def merge_piece(train, low, high, norm, index, rows, extra, after):
    rank, width = low.shape
    return pl.pallas_call(
        functools.partial(merge_kernel, tile=128),
        grid=(1,),
        in_specs=[
            pl.BlockSpec((width, rows), lambda i: (0, index)),
            pl.BlockSpec((rank, width), lambda i: (0, 0)),
            pl.BlockSpec((rank, rows), lambda i: (0, index)),
            pl.BlockSpec((1, width), lambda i: (0, 0)),
        ] + [ANY] * len(after),
        out_specs=pl.BlockSpec((rows + extra, width), lambda i: (0, 0)),
        out_shape=jax.ShapeDtypeStruct((rows + extra, width), jnp.bfloat16),
        cost_estimate=pl.CostEstimate(
            flops=2 * width * rank * rows, bytes_accessed=4 * width * rows, transcendentals=0
        ),
    )(train, low, high, norm, *after)


def flip(position, mask):
    bit = 1
    while bit <= mask:
        if mask & bit:
            position = position + bit - 2 * bit * ((position // bit) % 2)
        bit *= 2
    return position


def place_kernel(*refs, count, slots, rows, width, inputs):
    pieces = refs[:count]
    out = refs[inputs]
    buffer, in_sem, out_sem = refs[-3:]
    me = lax.axis_index("rows")

    def load(i):
        return pltpu.make_async_copy(pieces[i].at[pl.ds(0, rows), :], buffer.at[i], in_sem.at[i])

    def store(i):
        index, mask = slots[i]
        column = pl.multiple_of(flip(me, mask) * width, width)
        return pltpu.make_async_copy(
            buffer.at[i], out.at[pl.ds(index * rows, rows), pl.ds(column, width)], out_sem.at[i]
        )

    for i in range(count):
        load(i).start()
    for i in range(count):
        load(i).wait()
        store(i).start()
    for i in range(count):
        store(i).wait()


def place(out, pieces, slots, rows, width, shape):
    count = len(pieces)
    if width % 128:
        me = lax.axis_index("rows")
        out = jnp.zeros(shape, jnp.bfloat16) if out is None else out
        for piece, (index, mask) in zip(pieces, slots):
            out = lax.dynamic_update_slice(out, piece[:rows], (index * rows, flip(me, mask) * width))
        return out
    aliased = out is not None
    operands = list(pieces) + ([out] if aliased else [])
    return pl.pallas_call(
        functools.partial(
            place_kernel, count=count, slots=tuple(slots), rows=rows, width=width, inputs=len(operands)
        ),
        in_specs=[ANY] * len(operands),
        out_specs=ANY,
        out_shape=jax.ShapeDtypeStruct(shape, jnp.bfloat16),
        scratch_shapes=[
            pltpu.VMEM((count, rows, width), jnp.bfloat16),
            pltpu.SemaphoreType.DMA((count,)),
            pltpu.SemaphoreType.DMA((count,)),
        ],
        input_output_aliases={count: 0} if aliased else {},
        cost_estimate=pl.CostEstimate(flops=0, bytes_accessed=4 * count * rows * width, transcendentals=0),
    )(*operands)


def add_norm(train, step, after):
    def kernel(train_ref, step_ref, *refs):
        refs[-1][...] = (train_ref[...] + step_ref[...]).astype(jnp.bfloat16)

    vmem = pl.BlockSpec(memory_space=pltpu.VMEM)
    return pl.pallas_call(
        kernel,
        in_specs=[vmem, vmem] + [ANY] * len(after),
        out_specs=vmem,
        out_shape=jax.ShapeDtypeStruct((1, train.shape[0]), jnp.bfloat16),
        name="add_norm",
    )(train[None, :], step[None, :], *after)


def collect_norm(pieces, rows, n, width):
    if width % 128:
        gains = jnp.stack([piece[rows] for piece in pieces])
        return gains[lax.axis_index("rows") ^ jnp.arange(n)].reshape(1, -1)

    def kernel(*refs):
        out, buffer, sem = refs[n:]
        me = lax.axis_index("rows")
        copies = [
            pltpu.make_async_copy(refs[k].at[pl.ds(rows, 16), :], buffer.at[k], sem.at[k]) for k in range(n)
        ]
        for copy in copies:
            copy.start()
        for k, copy in enumerate(copies):
            copy.wait()
            column = pl.multiple_of(flip(me, k) * width, 128)
            out[:, pl.ds(column, width)] = buffer[k, 0:1, :]

    return pl.pallas_call(
        kernel,
        in_specs=[ANY] * n,
        out_specs=pl.BlockSpec(memory_space=pltpu.VMEM),
        out_shape=jax.ShapeDtypeStruct((1, n * width), jnp.bfloat16),
        scratch_shapes=[pltpu.VMEM((n, 16, width), jnp.bfloat16), pltpu.SemaphoreType.DMA((n,))],
        name="collect_norm",
    )(*pieces)


def per_device(train_up, low_up, high_up, norm_train, norm_step, *, n, t):
    width, m = train_up.shape
    pieces = max(p for p in range(1, PIECES + 1) if m % (128 * p) == 0)
    rows = m // pieces
    pairs = [list(range(i, min(i + 2, pieces))) for i in range(0, pieces, 2)]
    outer = [1 << b for b in range(1, n.bit_length() - 1)]
    low_up = low_up.T

    def swap(x, axis, size, mask):
        return lax.ppermute(x, axis, [(i, i ^ mask) for i in range(size)])

    def gather_norm(after):
        norm = add_norm(norm_train, norm_step, after)
        mine = lax.axis_index("tp")
        bit = 1
        while bit < t:
            other = swap(norm, "tp", t, bit)
            upper = (mine // bit) % 2 == 1
            norm = jnp.where(
                upper,
                jnp.concatenate([other, norm], axis=1),
                jnp.concatenate([norm, other], axis=1),
            )
            bit *= 2
        return norm

    dummy = jnp.zeros((1, width), jnp.bfloat16)
    norm_pair = max(len(pairs) - 2, 0)
    carrier = pairs[norm_pair][-1]
    held = {}
    for index in range(pieces):
        extra = 16 if index == carrier else 0
        norm = gather_norm([]) if extra else dummy
        held[index] = {0: merge_piece(train_up, low_up, high_up, norm, index, rows, extra, [])}

    early, late = [], []
    for pair in pairs:
        first, second = [], []
        for index in pair:
            have = held[index]
            k = index % max(len(outer), 1)
            order = outer[k:] + outer[:k]
            first.append((index, 0))
            for step, bit in enumerate(order):
                for mask in list(have):
                    final = step == len(order) - 1 and mask != 0
                    have[mask ^ bit] = swap(have[mask], "rows", n, bit)
                    (second if final else first).append((index, mask ^ bit))
        for group in (first, second):
            for index, mask in list(group):
                held[index][mask ^ 1] = swap(held[index][mask], "rows", n, 1)
                group.append((index, mask ^ 1))
        early.append(first)
        late.append(second)

    out = None
    for groups in (early, late):
        for group in groups:
            if group:
                out = place(out, [held[i][k] for i, k in group], group, rows, width, (m, n * width))
    serve_norm = collect_norm([held[carrier][k] for k in range(n)], rows, n, width)
    return out, serve_norm.reshape(-1)


def solution(mesh):
    placed = (P("rows", "tp"), P("rows", None), P(None, "tp"), P(("rows", "tp")), P(("rows", "tp")))
    body = functools.partial(per_device, n=mesh.shape["rows"], t=mesh.shape["tp"])
    return jax.shard_map(
        body, mesh=mesh, in_specs=placed, out_specs=(P("tp", None), P()), check_vma=False
    )
```

time: 339 us -> 291 us (0.86)
  local copies, waits for them, and re-layouts: 70.8 us -> 3.05 us
  Pallas kernels: 0 us -> 65.1 us
  blocking collectives: 42.7 us -> 0 us
  starting transfers between devices: 0.04 us -> 39.1 us
  waiting for transfers between devices: 201 us -> 179 us
  between operations: 14.1 us -> 0.93 us
  matrix products: 7.56 us -> 0 us
  other arithmetic: 0.01 us -> 3.68 us
    all_gather x1 -> x0, waiting for transfers between devices: 201 us -> none  [per_device(): ready_up = lax.all_gather(narrow_up, 'rows', axis=0, tiled=True)]
    ppermute x0 -> x58, waiting for transfers between devices: none -> 179 us  [swap(): return lax.ppermute(x, axis, [(i, i ^ mask) for i in range(size)])]
    unnamed x11 -> x62, local copies, waits for them, and re-layouts: 70.8 us -> 2.46 us
    pallas_call x0 -> x18, Pallas kernels: none -> 65.1 us  [the longest x8 42.1 us: place(): pl.pallas_call(functools.partial(place_kernel, count=count, slots=tuple(s...]
    unnamed x1 -> x0, blocking collectives: 42.7 us -> none
    ppermute x0 -> x58, starting transfers between devices: none -> 39.1 us  [swap(): return lax.ppermute(x, axis, [(i, i ^ mask) for i in range(size)])]
    dot_general x1 -> x0, matrix products: 7.56 us -> none  [per_device(): jnp.dot(low_up, high_up, preferred_element_type=jnp.float32)]
  transfers between devices with their start and end apart: 1 -> 58, of which waited for: 1 -> 27; matrix products, arithmetic and copies ran while one was open for 0% -> 1% of each run, Pallas kernels for 0% -> 21%
where the time goes in v1:
time: 291 us
  waiting for transfers between devices  179 us (62%)
  Pallas kernels  65.1 us (22%)
  starting transfers between devices  39.1 us (13%)
  other arithmetic  3.68 us (1%)
  local copies, waits for them, and re-layouts  3.05 us (1%)
    ppermute x58, waiting for transfers between devices, swap(): return lax.ppermute(x, axis, [(i, i ^ mask) for i in range(size)])  179 us
    pallas_call x8, Pallas kernels, place(): pl.pallas_call(functools.partial(place_kernel, count=count, slots=tuple(s...  42.1 us
    ppermute x58, starting transfers between devices, swap(): return lax.ppermute(x, axis, [(i, i ^ mask) for i in range(size)])  39.1 us
    pallas_call x8, Pallas kernels, merge_piece(): pl.pallas_call(functools.partial(merge_kernel, tile=128), grid=(1,), in_s...  20.3 us
  transfers between devices with their start and end apart: 58, of which 27 were waited for; matrix products, arithmetic and copies ran while one was open for 1% of the time, Pallas kernels for 21%

profile of v1, /device:TPU:0, one launch (start us, length us, event | category | flops | bytes accessed | tf_op | source)
XLA Modules:
  0.0 290.6 jit_solution(8710681693503939711)
XLA Ops:
  1.2 2.5 shard_map.74.refs_0_
  3.7 3.0 %collective-permute-start.20 = (bf16[640,640]{1,0:T(8,128)(2,1)}, bf16[640,640]{1,0:T(8,128)(2,1)S(1)}, u32[]{:S(2)}, u32[]{:S(2)}) collective-permute-start(bf16[640,640]{1,0:T(8,128)(2,1)} %shard_map.74.refs_0_), channel_id=1, source_target_pairs={{0,8},{4,12},{8,0},{12,4},{16,24},{20,28},{24,16},{28,20},{1,9},{5... | collective-permute-start | bytes 2457608 | tf_op jit(solution)/shard_map/ppermute | solution.py:161
  6.7 1.5 collective-permute-start.50
  8.2 2.5 shard_map.75.refs_3_
  12.5 2.1 collective-permute-start.8
  14.5 1.8 collective-permute-done.8
  17.1 3.0 %collective-permute-start.9 = (bf16[1,320]{1,0:T(2,128)(2,1)S(1)}, bf16[1,320]{1,0:T(2,128)(2,1)S(1)}, u32[]{:S(2)}, u32[]{:S(2)}) collective-permute-start(bf16[1,320]{1,0:T(2,128)(2,1)S(1)} %broadcast_select_fusion.1), channel_id=1, source_target_pairs={{0,2},{1,3},{2,0},{3,1},{4,6},{5,7},{6,4},{7,5},{8,10},{9,11},{10,... | collective-permute-start | bytes 1928 | tf_op jit(solution)/shard_map/ppermute | solution.py:161
  20.2 1.6 collective-permute-done.9
  21.8 4.2 %collective-permute-done.20.refs_1_ = bf16[640,640]{1,0:T(8,128)(2,1)S(1)} collective-permute-done((bf16[640,640]{1,0:T(8,128)(2,1)}, bf16[640,640]{1,0:T(8,128)(2,1)S(1)}, u32[]{:S(2)}, u32[]{:S(2)}) %collective-permute-start.20) | collective-permute-done | bytes 819232 | tf_op jit(solution)/shard_map/ppermute | solution.py:161
  26.0 2.8 shard_map.72.refs_0_
  28.8 15.4 %collective-permute-done.22.refs_4_ = bf16[640,640]{1,0:T(8,128)(2,1)S(1)} collective-permute-done((bf16[640,640]{1,0:T(8,128)(2,1)}, bf16[640,640]{1,0:T(8,128)(2,1)S(1)}, u32[]{:S(2)}, u32[]{:S(2)}) %collective-permute-start.22) | collective-permute-done | bytes 819232 | tf_op jit(solution)/shard_map/ppermute | solution.py:161
  44.5 2.5 shard_map.73.refs_3_
  47.0 1.7 collective-permute-start.16
  49.0 1.7 collective-permute-start.43
  50.7 14.9 %collective-permute-done.14.refs_1_ = bf16[640,640]{1,0:T(8,128)(2,1)} collective-permute-done((bf16[640,640]{1,0:T(8,128)(2,1)}, bf16[640,640]{1,0:T(8,128)(2,1)}, u32[]{:S(2)}, u32[]{:S(2)}) %collective-permute-start.14) | collective-permute-done | bytes 819232 | tf_op jit(solution)/shard_map/ppermute | solution.py:161
  65.6 2.5 shard_map.70.refs_0_
  68.4 1.7 collective-permute-start.6
  70.1 13.6 %collective-permute-done.42.refs_2_ = bf16[640,640]{1,0:T(8,128)(2,1)} collective-permute-done((bf16[640,640]{1,0:T(8,128)(2,1)}, bf16[640,640]{1,0:T(8,128)(2,1)}, u32[]{:S(2)}, u32[]{:S(2)}) %collective-permute-start.42) | collective-permute-done | bytes 819232 | tf_op jit(solution)/shard_map/ppermute | solution.py:161
  83.7 1.5 collective-permute-start.34
  85.2 2.6 shard_map.68.refs_0_
  87.7 1.5 collective-permute-start
  89.3 2.5 shard_map.69.refs_3_
  92.2 8.4 %collective-permute-done.6.refs_1_ = bf16[640,640]{1,0:T(8,128)(2,1)} collective-permute-done((bf16[640,640]{1,0:T(8,128)(2,1)}, bf16[640,640]{1,0:T(8,128)(2,1)}, u32[]{:S(2)}, u32[]{:S(2)}) %collective-permute-start.6) | collective-permute-done | bytes 819232 | tf_op jit(solution)/shard_map/ppermute | solution.py:161
  100.7 1.5 collective-permute-start.26
  102.2 2.8 collective-permute-done.34.refs_2_
  105.0 1.4 collective-permute-start.27
  106.4 11.8 %collective-permute-done.refs_1_ = bf16[640,640]{1,0:T(8,128)(2,1)} collective-permute-done((bf16[640,640]{1,0:T(8,128)(2,1)}, bf16[640,640]{1,0:T(8,128)(2,1)}, u32[]{:S(2)}, u32[]{:S(2)}) %collective-permute-start) | collective-permute-done | bytes 819232 | tf_op jit(solution)/shard_map/ppermute | solution.py:161
  119.7 2.5 shard_map.71.refs_3_.refs_0_
  122.7 1.5 collective-permute-start.10
  124.2 16.1 %collective-permute-done.26.refs_2_ = bf16[640,640]{1,0:T(8,128)(2,1)} collective-permute-done((bf16[640,640]{1,0:T(8,128)(2,1)}, bf16[640,640]{1,0:T(8,128)(2,1)}, u32[]{:S(2)}, u32[]{:S(2)}) %collective-permute-start.26) | collective-permute-done | bytes 819232 | tf_op jit(solution)/shard_map/ppermute | solution.py:161
  140.2 1.4 collective-permute-start.35
  142.2 12.8 %collective-permute-done.10.refs_4_ = bf16[656,640]{1,0:T(8,128)(2,1)S(1)} collective-permute-done((bf16[656,640]{1,0:T(8,128)(2,1)}, bf16[656,640]{1,0:T(8,128)(2,1)S(1)}, u32[]{:S(2)}, u32[]{:S(2)}) %collective-permute-start.10) | collective-permute-done | bytes 839712 | tf_op jit(solution)/shard_map/ppermute | solution.py:161
  156.1 1.4 collective-permute-done.54.refs_8_
  167.0 1.5 collective-permute-start.23
  171.9 15.2 %collective-permute-done.21.refs_0_ = bf16[640,640]{1,0:T(8,128)(2,1)S(1)} collective-permute-done((bf16[640,640]{1,0:T(8,128)(2,1)}, bf16[640,640]{1,0:T(8,128)(2,1)S(1)}, u32[]{:S(2)}, u32[]{:S(2)}) %collective-permute-start.21) | collective-permute-done | bytes 819232 | tf_op jit(solution)/shard_map/ppermute | solution.py:161
  189.5 15.2 %collective-permute-done.15.refs_0_ = bf16[640,640]{1,0:T(8,128)(2,1)S(1)} collective-permute-done((bf16[640,640]{1,0:T(8,128)(2,1)}, bf16[640,640]{1,0:T(8,128)(2,1)S(1)}, u32[]{:S(2)}, u32[]{:S(2)}) %collective-permute-start.15) | collective-permute-done | bytes 819232 | tf_op jit(solution)/shard_map/ppermute | solution.py:161
  206.7 15.6 %collective-permute-done.7.refs_0_ = bf16[640,640]{1,0:T(8,128)(2,1)} collective-permute-done((bf16[640,640]{1,0:T(8,128)(2,1)}, bf16[640,640]{1,0:T(8,128)(2,1)}, u32[]{:S(2)}, u32[]{:S(2)}) %collective-permute-start.7) | collective-permute-done | bytes 819232 | tf_op jit(solution)/shard_map/ppermute | solution.py:161
  222.3 16.7 %collective-permute-done.1.refs_0_ = bf16[640,640]{1,0:T(8,128)(2,1)} collective-permute-done((bf16[640,640]{1,0:T(8,128)(2,1)}, bf16[640,640]{1,0:T(8,128)(2,1)}, u32[]{:S(2)}, u32[]{:S(2)}) %collective-permute-start.1) | collective-permute-done | bytes 819232 | tf_op jit(solution)/shard_map/ppermute | solution.py:161
  239.7 2.0 collective-permute-done.11.refs_1_.refs_6_
  245.5 7.6 %shard_map.76.refs_12_ = bf16[5120,5120]{1,0:T(8,128)(2,1)} custom-call(bf16[640,640]{1,0:T(8,128)(2,1)} %shard_map.74.refs_0_, bf16[640,640]{1,0:T(8,128)(2,1)} %copy-done.15, bf16[640,640]{1,0:T(8,128)(2,1)} %copy-done.16, bf16[640,640]{1,0:T(8,128)(2,1)} %shard_map.75.refs_3_, bf16[640,640]{1,0:T(8,128)(2,1)} %copy-done.17, bf16[640,640]{1,0:T(8,128)(2,1)} %copy-done.18, ...), custom_call_target="tpu_custom_call" | custom-call | bytes 19660800 | tf_op jit(solution)/shard_map/pallas_call | solution.py:93
  253.1 7.6 %shard_map.77.refs_12_ = bf16[5120,5120]{1,0:T(8,128)(2,1)} custom-call(bf16[640,640]{1,0:T(8,128)(2,1)} %shard_map.72.refs_0_, bf16[640,640]{1,0:T(8,128)(2,1)} %collective-permute-done.14.refs_1_, bf16[640,640]{1,0:T(8,128)(2,1)} %collective-permute-done.42.refs_2_, bf16[640,640]{1,0:T(8,128)(2,1)} %shard_map.73.refs_3_, ...), custom_call_target="tpu_custom_call", output_to_operand_aliasing={{}: (12, {})} | custom-call | bytes 19660800 | tf_op jit(solution)/shard_map/pallas_call | solution.py:93
  260.7 7.6 %shard_map.78.refs_12_ = bf16[5120,5120]{1,0:T(8,128)(2,1)} custom-call(bf16[640,640]{1,0:T(8,128)(2,1)} %shard_map.70.refs_0_, bf16[640,640]{1,0:T(8,128)(2,1)} %collective-permute-done.6.refs_1_, bf16[640,640]{1,0:T(8,128)(2,1)} %copy-done.5, bf16[656,640]{1,0:T(8,128)(2,1)} %shard_map.71.refs_3_.refs_0_, ...), custom_call_target="tpu_custom_call", output_to_operand_aliasing={{}: (12, {})} | custom-call | bytes 19660800 | tf_op jit(solution)/shard_map/pallas_call | solution.py:93
  268.3 7.6 %shard_map.79.refs_4_ = bf16[5120,5120]{1,0:T(8,128)(2,1)} custom-call(bf16[640,640]{1,0:T(8,128)(2,1)} %shard_map.68.refs_0_, bf16[640,640]{1,0:T(8,128)(2,1)} %collective-permute-done.refs_1_, bf16[640,640]{1,0:T(8,128)(2,1)} %collective-permute-done.26.refs_2_, bf16[640,640]{1,0:T(8,128)(2,1)} %shard_map.69.refs_3_, ...), custom_call_target="tpu_custom_call", output_to_operand_aliasing={{}: (12, {})} | custom-call | bytes 19660800 | tf_op jit(solution)/shard_map/pallas_call | solution.py:93
  275.9 2.9 %shard_map.80.refs_4_ = bf16[5120,5120]{1,0:T(8,128)(2,1)} custom-call(bf16[640,640]{1,0:T(8,128)(2,1)} %copy-done.9, bf16[640,640]{1,0:T(8,128)(2,1)} %copy-done.11, bf16[640,640]{1,0:T(8,128)(2,1)} %copy-done.12, bf16[640,640]{1,0:T(8,128)(2,1)} %copy-done.14, bf16[5120,5120]{1,0:T(8,128)(2,1)} %shard_map.79.refs_4_), custom_call_target="tpu_custom_call", output_to_operand_aliasing={{}: (4, {})} | custom-call | bytes 6553600 | tf_op jit(solution)/shard_map/pallas_call | solution.py:93
  278.9 2.9 %shard_map.81.refs_4_ = bf16[5120,5120]{1,0:T(8,128)(2,1)} custom-call(bf16[640,640]{1,0:T(8,128)(2,1)} %copy-done.10, bf16[640,640]{1,0:T(8,128)(2,1)} %collective-permute-done.17.refs_1_, bf16[640,640]{1,0:T(8,128)(2,1)} %copy-done.13, bf16[640,640]{1,0:T(8,128)(2,1)} %collective-permute-done.19.refs_3_, ...), custom_call_target="tpu_custom_call", output_to_operand_aliasing={{}: (4, {})} | custom-call | bytes 6553600 | tf_op jit(solution)/shard_map/pallas_call | solution.py:93
  281.8 1.5 collect_norm.1
  284.7 2.9 %shard_map.82.refs_4_ = bf16[5120,5120]{1,0:T(8,128)(2,1)} custom-call(bf16[640,640]{1,0:T(8,128)(2,1)} %collective-permute-done.7.refs_0_, bf16[656,640]{1,0:T(8,128)(2,1)} %collective-permute-done.11.refs_1_.refs_6_, bf16[640,640]{1,0:T(8,128)(2,1)} %collective-permute-done.12.refs_2_, ...), custom_call_target="tpu_custom_call", output_to_operand_aliasing={{}: (4, {})} | custom-call | bytes 6553600 | tf_op jit(solution)/shard_map/pallas_call | solution.py:93
  287.6 2.9 %shard_map.83 = bf16[5120,5120]{1,0:T(8,128)(2,1)} custom-call(bf16[640,640]{1,0:T(8,128)(2,1)} %collective-permute-done.1.refs_0_, bf16[640,640]{1,0:T(8,128)(2,1)} %collective-permute-done.3.refs_1_, bf16[640,640]{1,0:T(8,128)(2,1)} %collective-permute-done.4.refs_2_, ...), custom_call_target="tpu_custom_call", output_to_operand_aliasing={{}: (4, {})} | custom-call | bytes 6553600 | tf_op jit(solution)/shard_map/pallas_call | solution.py:93
  (156 shorter events, 31.5 us)
Async XLA Ops:
  3.7 22.3 %collective-permute-start.20 = (bf16[640,640]{1,0:T(8,128)(2,1)}, bf16[640,640]{1,0:T(8,128)(2,1)S(1)}, u32[]{:S(2)}, u32[]{:S(2)}) collective-permute-start(bf16[640,640]{1,0:T(8,128)(2,1)} %shard_map.74.refs_0_), channel_id=1, source_target_pairs={{0,8},{4,12},{8,0},{12,4},{16,24},{20,28},{24,16},{28,20},{1,9},{5... | collective-permute-start | bytes 2457608 | tf_op jit(solution)/shard_map/ppermute | solution.py:161
  6.7 40.3 %collective-permute-start.50 = (bf16[640,640]{1,0:T(8,128)(2,1)}, bf16[640,640]{1,0:T(8,128)(2,1)S(1)}, u32[]{:S(2)}, u32[]{:S(2)}) collective-permute-start(bf16[640,640]{1,0:T(8,128)(2,1)} %shard_map.74.refs_0_), channel_id=1, source_target_pairs={{0,16},{4,20},{8,24},{12,28},{16,0},{20,4},{24,8},{28,12},{1,17},{... | collective-permute-start | bytes 2457608 | tf_op jit(solution)/shard_map/ppermute | solution.py:161
  10.7 33.5 %collective-permute-start.22 = (bf16[640,640]{1,0:T(8,128)(2,1)}, bf16[640,640]{1,0:T(8,128)(2,1)S(1)}, u32[]{:S(2)}, u32[]{:S(2)}) collective-permute-start(bf16[640,640]{1,0:T(8,128)(2,1)} %shard_map.75.refs_3_), channel_id=1, source_target_pairs={{0,16},{4,20},{8,24},{12,28},{16,0},{20,4},{24,8},{28,12},{1,17},{... | collective-permute-start | bytes 2457608 | tf_op jit(solution)/shard_map/ppermute | solution.py:161
  11.2 37.5 %collective-permute-start.51 = (bf16[640,640]{1,0:T(8,128)(2,1)}, bf16[640,640]{1,0:T(8,128)(2,1)S(1)}, u32[]{:S(2)}, u32[]{:S(2)}) collective-permute-start(bf16[640,640]{1,0:T(8,128)(2,1)} %shard_map.75.refs_3_), channel_id=1, source_target_pairs={{0,8},{4,12},{8,0},{12,4},{16,24},{20,28},{24,16},{28,20},{1,9},{5... | collective-permute-start | bytes 2457608 | tf_op jit(solution)/shard_map/ppermute | solution.py:161
  21.7 27.3 %collective-permute-start.52 = (bf16[640,640]{1,0:T(8,128)(2,1)}, bf16[640,640]{1,0:T(8,128)(2,1)}, u32[]{:S(2)}, u32[]{:S(2)}) collective-permute-start(bf16[640,640]{1,0:T(8,128)(2,1)} %shard_map.74.refs_0_), channel_id=1, source_target_pairs={{0,4},{4,0},{8,12},{12,8},{16,20},{20,16},{24,28},{28,24},{1,5},{5... | collective-permute-start | bytes 2457608 | tf_op jit(solution)/shard_map/ppermute | solution.py:161
  26.0 24.7 %collective-permute-start.55 = (bf16[640,640]{1,0:T(8,128)(2,1)}, bf16[640,640]{1,0:T(8,128)(2,1)}, u32[]{:S(2)}, u32[]{:S(2)}) collective-permute-start(bf16[640,640]{1,0:T(8,128)(2,1)} %shard_map.75.refs_3_), channel_id=1, source_target_pairs={{0,4},{4,0},{8,12},{12,8},{16,20},{20,16},{24,28},{28,24},{1,5},{5... | collective-permute-start | bytes 2457608 | tf_op jit(solution)/shard_map/ppermute | solution.py:161
  44.1 21.4 %collective-permute-start.14 = (bf16[640,640]{1,0:T(8,128)(2,1)}, bf16[640,640]{1,0:T(8,128)(2,1)}, u32[]{:S(2)}, u32[]{:S(2)}) collective-permute-start(bf16[640,640]{1,0:T(8,128)(2,1)} %shard_map.72.refs_0_), channel_id=1, source_target_pairs={{0,8},{4,12},{8,0},{12,4},{16,24},{20,28},{24,16},{28,20},{1,9},{5... | collective-permute-start | bytes 2457608 | tf_op jit(solution)/shard_map/ppermute | solution.py:161
  47.0 21.4 %collective-permute-start.16 = (bf16[640,640]{1,0:T(8,128)(2,1)}, bf16[640,640]{1,0:T(8,128)(2,1)}, u32[]{:S(2)}, u32[]{:S(2)}) collective-permute-start(bf16[640,640]{1,0:T(8,128)(2,1)} %shard_map.73.refs_3_), channel_id=1, source_target_pairs={{0,16},{4,20},{8,24},{12,28},{16,0},{20,4},{24,8},{28,12},{1,17},{... | collective-permute-start | bytes 2457608 | tf_op jit(solution)/shard_map/ppermute | solution.py:161
  48.7 35.0 %collective-permute-start.42 = (bf16[640,640]{1,0:T(8,128)(2,1)}, bf16[640,640]{1,0:T(8,128)(2,1)}, u32[]{:S(2)}, u32[]{:S(2)}) collective-permute-start(bf16[640,640]{1,0:T(8,128)(2,1)} %shard_map.72.refs_0_), channel_id=1, source_target_pairs={{0,16},{4,20},{8,24},{12,28},{16,0},{20,4},{24,8},{28,12},{1,17},{... | collective-permute-start | bytes 2457608 | tf_op jit(solution)/shard_map/ppermute | solution.py:161
  49.0 38.7 %collective-permute-start.43 = (bf16[640,640]{1,0:T(8,128)(2,1)}, bf16[640,640]{1,0:T(8,128)(2,1)}, u32[]{:S(2)}, u32[]{:S(2)}) collective-permute-start(bf16[640,640]{1,0:T(8,128)(2,1)} %shard_map.73.refs_3_), channel_id=1, source_target_pairs={{0,8},{4,12},{8,0},{12,4},{16,24},{20,28},{24,16},{28,20},{1,9},{5... | collective-permute-start | bytes 2457608 | tf_op jit(solution)/shard_map/ppermute | solution.py:161
  50.7 37.0 %collective-permute-start.44 = (bf16[640,640]{1,0:T(8,128)(2,1)}, bf16[640,640]{1,0:T(8,128)(2,1)}, u32[]{:S(2)}, u32[]{:S(2)}) collective-permute-start(bf16[640,640]{1,0:T(8,128)(2,1)} %shard_map.72.refs_0_), channel_id=1, source_target_pairs={{0,4},{4,0},{8,12},{12,8},{16,20},{20,16},{24,28},{28,24},{1,5},{5... | collective-permute-start | bytes 2457608 | tf_op jit(solution)/shard_map/ppermute | solution.py:161
  65.6 26.2 %collective-permute-start.47 = (bf16[640,640]{1,0:T(8,128)(2,1)}, bf16[640,640]{1,0:T(8,128)(2,1)}, u32[]{:S(2)}, u32[]{:S(2)}) collective-permute-start(bf16[640,640]{1,0:T(8,128)(2,1)} %shard_map.73.refs_3_), channel_id=1, source_target_pairs={{0,4},{4,0},{8,12},{12,8},{16,20},{20,16},{24,28},{28,24},{1,5},{5... | collective-permute-start | bytes 2457608 | tf_op jit(solution)/shard_map/ppermute | solution.py:161
  68.4 32.3 %collective-permute-start.6 = (bf16[640,640]{1,0:T(8,128)(2,1)}, bf16[640,640]{1,0:T(8,128)(2,1)}, u32[]{:S(2)}, u32[]{:S(2)}) collective-permute-start(bf16[640,640]{1,0:T(8,128)(2,1)} %shard_map.70.refs_0_), channel_id=1, source_target_pairs={{0,8},{4,12},{8,0},{12,4},{16,24},{20,28},{24,16},{28,20},{1,9},{5... | collective-permute-start | bytes 2457608 | tf_op jit(solution)/shard_map/ppermute | solution.py:161
  83.7 21.3 %collective-permute-start.34 = (bf16[640,640]{1,0:T(8,128)(2,1)}, bf16[640,640]{1,0:T(8,128)(2,1)S(1)}, u32[]{:S(2)}, u32[]{:S(2)}) collective-permute-start(bf16[640,640]{1,0:T(8,128)(2,1)} %shard_map.70.refs_0_), channel_id=1, source_target_pairs={{0,16},{4,20},{8,24},{12,28},{16,0},{20,4},{24,8},{28,12},{1,17},{... | collective-permute-start | bytes 2457608 | tf_op jit(solution)/shard_map/ppermute | solution.py:161
  87.7 18.7 %collective-permute-start.36 = (bf16[640,640]{1,0:T(8,128)(2,1)}, bf16[640,640]{1,0:T(8,128)(2,1)S(1)}, u32[]{:S(2)}, u32[]{:S(2)}) collective-permute-start(bf16[640,640]{1,0:T(8,128)(2,1)} %shard_map.70.refs_0_), channel_id=1, source_target_pairs={{0,4},{4,0},{8,12},{12,8},{16,20},{20,16},{24,28},{28,24},{1,5},{5... | collective-permute-start | bytes 2457608 | tf_op jit(solution)/shard_map/ppermute | solution.py:161
  87.7 30.5 %collective-permute-start = (bf16[640,640]{1,0:T(8,128)(2,1)}, bf16[640,640]{1,0:T(8,128)(2,1)}, u32[]{:S(2)}, u32[]{:S(2)}) collective-permute-start(bf16[640,640]{1,0:T(8,128)(2,1)} %shard_map.68.refs_0_), channel_id=1, source_target_pairs={{0,8},{4,12},{8,0},{12,4},{16,24},{20,28},{24,16},{28,20},{1,9},{5... | collective-permute-start | bytes 2457608 | tf_op jit(solution)/shard_map/ppermute | solution.py:161
  91.7 30.9 %collective-permute-start.2 = (bf16[640,640]{1,0:T(8,128)(2,1)}, bf16[640,640]{1,0:T(8,128)(2,1)}, u32[]{:S(2)}, u32[]{:S(2)}) collective-permute-start(bf16[640,640]{1,0:T(8,128)(2,1)} %shard_map.69.refs_3_), channel_id=1, source_target_pairs={{0,16},{4,20},{8,24},{12,28},{16,0},{20,4},{24,8},{28,12},{1,17},{... | collective-permute-start | bytes 2457608 | tf_op jit(solution)/shard_map/ppermute | solution.py:161
  100.7 39.6 %collective-permute-start.26 = (bf16[640,640]{1,0:T(8,128)(2,1)}, bf16[640,640]{1,0:T(8,128)(2,1)}, u32[]{:S(2)}, u32[]{:S(2)}) collective-permute-start(bf16[640,640]{1,0:T(8,128)(2,1)} %shard_map.68.refs_0_), channel_id=1, source_target_pairs={{0,16},{4,20},{8,24},{12,28},{16,0},{20,4},{24,8},{28,12},{1,17},{... | collective-permute-start | bytes 2457608 | tf_op jit(solution)/shard_map/ppermute | solution.py:161
  105.0 36.6 %collective-permute-start.27 = (bf16[640,640]{1,0:T(8,128)(2,1)}, bf16[640,640]{1,0:T(8,128)(2,1)}, u32[]{:S(2)}, u32[]{:S(2)}) collective-permute-start(bf16[640,640]{1,0:T(8,128)(2,1)} %shard_map.69.refs_3_), channel_id=1, source_target_pairs={{0,8},{4,12},{8,0},{12,4},{16,24},{20,28},{24,16},{28,20},{1,9},{5... | collective-permute-start | bytes 2457608 | tf_op jit(solution)/shard_map/ppermute | solution.py:161
  106.4 35.2 %collective-permute-start.28 = (bf16[640,640]{1,0:T(8,128)(2,1)}, bf16[640,640]{1,0:T(8,128)(2,1)}, u32[]{:S(2)}, u32[]{:S(2)}) collective-permute-start(bf16[640,640]{1,0:T(8,128)(2,1)} %shard_map.68.refs_0_), channel_id=1, source_target_pairs={{0,4},{4,0},{8,12},{12,8},{16,20},{20,16},{24,28},{28,24},{1,5},{5... | collective-permute-start | bytes 2457608 | tf_op jit(solution)/shard_map/ppermute | solution.py:161
  118.2 23.9 %collective-permute-start.31 = (bf16[640,640]{1,0:T(8,128)(2,1)}, bf16[640,640]{1,0:T(8,128)(2,1)}, u32[]{:S(2)}, u32[]{:S(2)}) collective-permute-start(bf16[640,640]{1,0:T(8,128)(2,1)} %shard_map.69.refs_3_), channel_id=1, source_target_pairs={{0,4},{4,0},{8,12},{12,8},{16,20},{20,16},{24,28},{28,24},{1,5},{5... | collective-permute-start | bytes 2457608 | tf_op jit(solution)/shard_map/ppermute | solution.py:161
  122.7 32.3 %collective-permute-start.10 = (bf16[656,640]{1,0:T(8,128)(2,1)}, bf16[656,640]{1,0:T(8,128)(2,1)S(1)}, u32[]{:S(2)}, u32[]{:S(2)}) collective-permute-start(bf16[656,640]{1,0:T(8,128)(2,1)} %shard_map.71.refs_3_.refs_0_), channel_id=1, source_target_pairs={{0,16},{4,20},{8,24},{12,28},{16,0},{20,4},{24,8},{28,12},{1,17},{... | collective-permute-start | bytes 2519048 | tf_op jit(solution)/shard_map/ppermute | solution.py:161
  140.2 14.8 %collective-permute-start.35 = (bf16[656,640]{1,0:T(8,128)(2,1)}, bf16[656,640]{1,0:T(8,128)(2,1)S(1)}, u32[]{:S(2)}, u32[]{:S(2)}) collective-permute-start(bf16[656,640]{1,0:T(8,128)(2,1)} %shard_map.71.refs_3_.refs_0_), channel_id=1, source_target_pairs={{0,8},{4,12},{8,0},{12,4},{16,24},{20,28},{24,16},{28,20},{1,9},{5... | collective-permute-start | bytes 2519048 | tf_op jit(solution)/shard_map/ppermute | solution.py:161
  141.6 13.9 %collective-permute-start.39 = (bf16[656,640]{1,0:T(8,128)(2,1)}, bf16[656,640]{1,0:T(8,128)(2,1)S(1)}, u32[]{:S(2)}, u32[]{:S(2)}) collective-permute-start(bf16[656,640]{1,0:T(8,128)(2,1)} %shard_map.71.refs_3_.refs_0_), channel_id=1, source_target_pairs={{0,4},{4,0},{8,12},{12,8},{16,20},{20,16},{24,28},{28,24},{1,5},{5... | collective-permute-start | bytes 2519048 | tf_op jit(solution)/shard_map/ppermute | solution.py:161
  141.7 14.0 %collective-permute-start.53 = (bf16[640,640]{1,0:T(8,128)(2,1)}, bf16[640,640]{1,0:T(8,128)(2,1)S(1)}, u32[]{:S(2)}, u32[]{:S(2)}) collective-permute-start(bf16[640,640]{1,0:T(8,128)(2,1)} %copy-done.15), channel_id=1, source_target_pairs={{0,4},{4,0},{8,12},{12,8},{16,20},{20,16},{24,28},{28,24},{1,5},{5... | collective-permute-start | bytes 2457608 | tf_op jit(solution)/shard_map/ppermute | solution.py:161
  142.2 13.9 %collective-permute-start.56 = (bf16[640,640]{1,0:T(8,128)(2,1)}, bf16[640,640]{1,0:T(8,128)(2,1)S(1)}, u32[]{:S(2)}, u32[]{:S(2)}) collective-permute-start(bf16[640,640]{1,0:T(8,128)(2,1)} %copy-done.17), channel_id=1, source_target_pairs={{0,4},{4,0},{8,12},{12,8},{16,20},{20,16},{24,28},{28,24},{1,5},{5... | collective-permute-start | bytes 2457608 | tf_op jit(solution)/shard_map/ppermute | solution.py:161
  156.0 6.2 %collective-permute-start.46 = (bf16[640,640]{1,0:T(8,128)(2,1)}, bf16[640,640]{1,0:T(8,128)(2,1)S(1)}, u32[]{:S(2)}, u32[]{:S(2)}) collective-permute-start(bf16[640,640]{1,0:T(8,128)(2,1)} %collective-permute-done.42.refs_2_), channel_id=1, source_target_pairs={{0,4},{4,0},{8,12},{12,8},{16,20},{20,16},{24,28},{28,24},{1,5},{5... | collective-permute-start | bytes 2457608 | tf_op jit(solution)/shard_map/ppermute | solution.py:161
  157.5 5.9 %collective-permute-start.49 = (bf16[640,640]{1,0:T(8,128)(2,1)}, bf16[640,640]{1,0:T(8,128)(2,1)S(1)}, u32[]{:S(2)}, u32[]{:S(2)}) collective-permute-start(bf16[640,640]{1,0:T(8,128)(2,1)} %collective-permute-done.43.refs_5_), channel_id=1, source_target_pairs={{0,4},{4,0},{8,12},{12,8},{16,20},{20,16},{24,28},{28,24},{1,5},{5... | collective-permute-start | bytes 2457608 | tf_op jit(solution)/shard_map/ppermute | solution.py:161
  158.7 5.9 %collective-permute-start.37 = (bf16[640,640]{1,0:T(8,128)(2,1)}, bf16[640,640]{1,0:T(8,128)(2,1)S(1)}, u32[]{:S(2)}, u32[]{:S(2)}) collective-permute-start(bf16[640,640]{1,0:T(8,128)(2,1)} %collective-permute-done.6.refs_1_), channel_id=1, source_target_pairs={{0,4},{4,0},{8,12},{12,8},{16,20},{20,16},{24,28},{28,24},{1,5},{5... | collective-permute-start | bytes 2457608 | tf_op jit(solution)/shard_map/ppermute | solution.py:161
  161.1 5.9 %collective-permute-start.29 = (bf16[640,640]{1,0:T(8,128)(2,1)}, bf16[640,640]{1,0:T(8,128)(2,1)S(1)}, u32[]{:S(2)}, u32[]{:S(2)}) collective-permute-start(bf16[640,640]{1,0:T(8,128)(2,1)} %collective-permute-done.refs_1_), channel_id=1, source_target_pairs={{0,4},{4,0},{8,12},{12,8},{16,20},{20,16},{24,28},{28,24},{1,5},{5... | collective-permute-start | bytes 2457608 | tf_op jit(solution)/shard_map/ppermute | solution.py:161
  162.2 6.2 %collective-permute-start.32 = (bf16[640,640]{1,0:T(8,128)(2,1)}, bf16[640,640]{1,0:T(8,128)(2,1)S(1)}, u32[]{:S(2)}, u32[]{:S(2)}) collective-permute-start(bf16[640,640]{1,0:T(8,128)(2,1)} %collective-permute-done.2.refs_4_), channel_id=1, source_target_pairs={{0,4},{4,0},{8,12},{12,8},{16,20},{20,16},{24,28},{28,24},{1,5},{5... | collective-permute-start | bytes 2457608 | tf_op jit(solution)/shard_map/ppermute | solution.py:161
  163.4 6.2 %collective-permute-start.30 = (bf16[640,640]{1,0:T(8,128)(2,1)}, bf16[640,640]{1,0:T(8,128)(2,1)S(1)}, u32[]{:S(2)}, u32[]{:S(2)}) collective-permute-start(bf16[640,640]{1,0:T(8,128)(2,1)} %collective-permute-done.26.refs_2_), channel_id=1, source_target_pairs={{0,4},{4,0},{8,12},{12,8},{16,20},{20,16},{24,28},{28,24},{1,5},{5... | collective-permute-start | bytes 2457608 | tf_op jit(solution)/shard_map/ppermute | solution.py:161
  164.6 6.2 %collective-permute-start.33 = (bf16[640,640]{1,0:T(8,128)(2,1)}, bf16[640,640]{1,0:T(8,128)(2,1)S(1)}, u32[]{:S(2)}, u32[]{:S(2)}) collective-permute-start(bf16[640,640]{1,0:T(8,128)(2,1)} %collective-permute-done.27.refs_5_), channel_id=1, source_target_pairs={{0,4},{4,0},{8,12},{12,8},{16,20},{20,16},{24,28},{28,24},{1,5},{5... | collective-permute-start | bytes 2457608 | tf_op jit(solution)/shard_map/ppermute | solution.py:161
  165.8 21.3 %collective-permute-start.21 = (bf16[640,640]{1,0:T(8,128)(2,1)}, bf16[640,640]{1,0:T(8,128)(2,1)S(1)}, u32[]{:S(2)}, u32[]{:S(2)}) collective-permute-start(bf16[640,640]{1,0:T(8,128)(2,1)} %copy-done.15), channel_id=1, source_target_pairs={{0,16},{4,20},{8,24},{12,28},{16,0},{20,4},{24,8},{28,12},{1,17},{... | collective-permute-start | bytes 2457608 | tf_op jit(solution)/shard_map/ppermute | solution.py:161
  167.0 21.4 %collective-permute-start.23 = (bf16[640,640]{1,0:T(8,128)(2,1)}, bf16[640,640]{1,0:T(8,128)(2,1)S(1)}, u32[]{:S(2)}, u32[]{:S(2)}) collective-permute-start(bf16[640,640]{1,0:T(8,128)(2,1)} %copy-done.17), channel_id=1, source_target_pairs={{0,8},{4,12},{8,0},{12,4},{16,24},{20,28},{24,16},{28,20},{1,9},{5... | collective-permute-start | bytes 2457608 | tf_op jit(solution)/shard_map/ppermute | solution.py:161
  168.5 36.2 %collective-permute-start.15 = (bf16[640,640]{1,0:T(8,128)(2,1)}, bf16[640,640]{1,0:T(8,128)(2,1)S(1)}, u32[]{:S(2)}, u32[]{:S(2)}) collective-permute-start(bf16[640,640]{1,0:T(8,128)(2,1)} %collective-permute-done.14.refs_1_), channel_id=1, source_target_pairs={{0,16},{4,20},{8,24},{12,28},{16,0},{20,4},{24,8},{28,12},{1,17},{... | collective-permute-start | bytes 2457608 | tf_op jit(solution)/shard_map/ppermute | solution.py:161
  169.6 36.1 %collective-permute-start.17 = (bf16[640,640]{1,0:T(8,128)(2,1)}, bf16[640,640]{1,0:T(8,128)(2,1)}, u32[]{:S(2)}, u32[]{:S(2)}) collective-permute-start(bf16[640,640]{1,0:T(8,128)(2,1)} %collective-permute-done.16.refs_4_), channel_id=1, source_target_pairs={{0,8},{4,12},{8,0},{12,4},{16,24},{20,28},{24,16},{28,20},{1,9},{5... | collective-permute-start | bytes 2457608 | tf_op jit(solution)/shard_map/ppermute | solution.py:161
  170.8 51.5 %collective-permute-start.7 = (bf16[640,640]{1,0:T(8,128)(2,1)}, bf16[640,640]{1,0:T(8,128)(2,1)}, u32[]{:S(2)}, u32[]{:S(2)}) collective-permute-start(bf16[640,640]{1,0:T(8,128)(2,1)} %collective-permute-done.6.refs_1_), channel_id=1, source_target_pairs={{0,16},{4,20},{8,24},{12,28},{16,0},{20,4},{24,8},{28,12},{1,17},{... | collective-permute-start | bytes 2457608 | tf_op jit(solution)/shard_map/ppermute | solution.py:161
  187.1 52.5 %collective-permute-start.40 = (bf16[656,640]{1,0:T(8,128)(2,1)S(1)}, bf16[656,640]{1,0:T(8,128)(2,1)S(1)}, u32[]{:S(2)}, u32[]{:S(2)}) collective-permute-start(bf16[656,640]{1,0:T(8,128)(2,1)S(1)} %collective-permute-done.10.refs_4_), channel_id=1, source_target_pairs={{0,4},{4,0},{8,12},{12,8},{16,20},{20,16},{24,28},{28,24},{1,5},{5... | collective-permute-start | bytes 2519048 | tf_op jit(solution)/shard_map/ppermute | solution.py:161
  188.4 50.6 %collective-permute-start.1 = (bf16[640,640]{1,0:T(8,128)(2,1)}, bf16[640,640]{1,0:T(8,128)(2,1)}, u32[]{:S(2)}, u32[]{:S(2)}) collective-permute-start(bf16[640,640]{1,0:T(8,128)(2,1)} %collective-permute-done.refs_1_), channel_id=1, source_target_pairs={{0,16},{4,20},{8,24},{12,28},{16,0},{20,4},{24,8},{28,12},{1,17},{... | collective-permute-start | bytes 2457608 | tf_op jit(solution)/shard_map/ppermute | solution.py:161
  204.6 34.4 %collective-permute-start.3 = (bf16[640,640]{1,0:T(8,128)(2,1)}, bf16[640,640]{1,0:T(8,128)(2,1)}, u32[]{:S(2)}, u32[]{:S(2)}) collective-permute-start(bf16[640,640]{1,0:T(8,128)(2,1)} %collective-permute-done.2.refs_4_), channel_id=1, source_target_pairs={{0,8},{4,12},{8,0},{12,4},{16,24},{20,28},{24,16},{28,20},{1,9},{5... | collective-permute-start | bytes 2457608 | tf_op jit(solution)/shard_map/ppermute | solution.py:161
  205.8 35.9 %collective-permute-start.11 = (bf16[656,640]{1,0:T(8,128)(2,1)S(1)}, bf16[656,640]{1,0:T(8,128)(2,1)}, u32[]{:S(2)}, u32[]{:S(2)}) collective-permute-start(bf16[656,640]{1,0:T(8,128)(2,1)S(1)} %collective-permute-done.10.refs_4_), channel_id=1, source_target_pairs={{0,8},{4,12},{8,0},{12,4},{16,24},{20,28},{24,16},{28,20},{1,9},{5... | collective-permute-start | bytes 2519048 | tf_op jit(solution)/shard_map/ppermute | solution.py:161
  222.3 19.4 %collective-permute-start.41 = (bf16[656,640]{1,0:T(8,128)(2,1)S(1)}, bf16[656,640]{1,0:T(8,128)(2,1)S(1)}, u32[]{:S(2)}, u32[]{:S(2)}) collective-permute-start(bf16[656,640]{1,0:T(8,128)(2,1)S(1)} %collective-permute-done.35.refs_5_.refs_2_), channel_id=1, source_target_pairs={{0,4},{4,0},{8,12},{12,8},{16,20},{20,16},{24,28},{28,24},{1,5},{5... | collective-permute-start | bytes 2519048 | tf_op jit(solution)/shard_map/ppermute | solution.py:161
  241.7 40.1 %collective-permute-start.13 = (bf16[656,640]{1,0:T(8,128)(2,1)}, bf16[656,640]{1,0:T(8,128)(2,1)}, u32[]{:S(2)}, u32[]{:S(2)}) collective-permute-start(bf16[656,640]{1,0:T(8,128)(2,1)} %collective-permute-done.11.refs_1_.refs_6_), channel_id=1, source_target_pairs={{0,4},{4,0},{8,12},{12,8},{16,20},{20,16},{24,28},{28,24},{1,5},{5... | collective-permute-start | bytes 2519048 | tf_op jit(solution)/shard_map/ppermute | solution.py:161
  242.6 36.3 %collective-permute-start.19 = (bf16[640,640]{1,0:T(8,128)(2,1)}, bf16[640,640]{1,0:T(8,128)(2,1)}, u32[]{:S(2)}, u32[]{:S(2)}) collective-permute-start(bf16[640,640]{1,0:T(8,128)(2,1)} %collective-permute-done.17.refs_1_), channel_id=1, source_target_pairs={{0,4},{4,0},{8,12},{12,8},{16,20},{20,16},{24,28},{28,24},{1,5},{5... | collective-permute-start | bytes 2457608 | tf_op jit(solution)/shard_map/ppermute | solution.py:161
  243.1 41.6 %collective-permute-start.12 = (bf16[640,640]{1,0:T(8,128)(2,1)}, bf16[640,640]{1,0:T(8,128)(2,1)}, u32[]{:S(2)}, u32[]{:S(2)}) collective-permute-start(bf16[640,640]{1,0:T(8,128)(2,1)} %collective-permute-done.7.refs_0_), channel_id=1, source_target_pairs={{0,4},{4,0},{8,12},{12,8},{16,20},{20,16},{24,28},{28,24},{1,5},{5... | collective-permute-start | bytes 2457608 | tf_op jit(solution)/shard_map/ppermute | solution.py:161
  243.2 44.4 %collective-permute-start.4 = (bf16[640,640]{1,0:T(8,128)(2,1)}, bf16[640,640]{1,0:T(8,128)(2,1)}, u32[]{:S(2)}, u32[]{:S(2)}) collective-permute-start(bf16[640,640]{1,0:T(8,128)(2,1)} %collective-permute-done.1.refs_0_), channel_id=1, source_target_pairs={{0,4},{4,0},{8,12},{12,8},{16,20},{20,16},{24,28},{28,24},{1,5},{5... | collective-permute-start | bytes 2457608 | tf_op jit(solution)/shard_map/ppermute | solution.py:161
  245.2 42.5 %collective-permute-start.5 = (bf16[640,640]{1,0:T(8,128)(2,1)}, bf16[640,640]{1,0:T(8,128)(2,1)}, u32[]{:S(2)}, u32[]{:S(2)}) collective-permute-start(bf16[640,640]{1,0:T(8,128)(2,1)} %collective-permute-done.3.refs_1_), channel_id=1, source_target_pairs={{0,4},{4,0},{8,12},{12,8},{16,20},{20,16},{24,28},{28,24},{1,5},{5... | collective-permute-start | bytes 2457608 | tf_op jit(solution)/shard_map/ppermute | solution.py:161
  (41 other events, 1480.0 us)

commit v2 on v1

--- a/solution.py
+++ b/solution.py
@@ -13,7 +13,7 @@
 ANY = pl.BlockSpec(memory_space=pl.ANY)
 
 
-def merge_kernel(train_ref, low_ref, high_ref, norm_ref, *refs, tile):
+def merge_kernel(train_ref, low_ref, high_ref, *refs, tile):
     piece_ref = refs[-1]
     rows = train_ref.shape[1]
     for start in range(0, rows, tile):
@@ -23,11 +23,13 @@
         )
         latest = train_ref[:, cols].T.astype(jnp.float32) + mix_rate * update
         piece_ref[cols, :] = latest.astype(jnp.bfloat16)
-    if piece_ref.shape[0] > rows:
+    if len(refs) > 1:
+        norm_ref = refs[0]
         piece_ref[rows:, :] = jnp.broadcast_to(norm_ref[...], (piece_ref.shape[0] - rows, norm_ref.shape[1]))
 
 
-def merge_piece(train, low, high, norm, index, rows, extra, after):
+def merge_piece(train, low, high, norm, index, rows):
+    extra = 0 if norm is None else 16
     rank, width = low.shape
     return pl.pallas_call(
         functools.partial(merge_kernel, tile=128),
@@ -36,14 +38,13 @@
             pl.BlockSpec((width, rows), lambda i: (0, index)),
             pl.BlockSpec((rank, width), lambda i: (0, 0)),
             pl.BlockSpec((rank, rows), lambda i: (0, index)),
-            pl.BlockSpec((1, width), lambda i: (0, 0)),
-        ] + [ANY] * len(after),
+        ] + ([] if norm is None else [pl.BlockSpec((1, width), lambda i: (0, 0))]),
         out_specs=pl.BlockSpec((rows + extra, width), lambda i: (0, 0)),
         out_shape=jax.ShapeDtypeStruct((rows + extra, width), jnp.bfloat16),
         cost_estimate=pl.CostEstimate(
             flops=2 * width * rank * rows, bytes_accessed=4 * width * rows, transcendentals=0
         ),
-    )(train, low, high, norm, *after)
+    )(train, low, high, *([] if norm is None else [norm]))
 
 
 def flip(position, mask):
@@ -107,18 +108,18 @@
     )(*operands)
 
 
-def add_norm(train, step, after):
-    def kernel(train_ref, step_ref, *refs):
-        refs[-1][...] = (train_ref[...] + step_ref[...]).astype(jnp.bfloat16)
+def add_norm(train, step):
+    def kernel(train_ref, step_ref, out_ref):
+        out_ref[...] = (train_ref[...] + step_ref[...]).astype(jnp.bfloat16)
 
     vmem = pl.BlockSpec(memory_space=pltpu.VMEM)
     return pl.pallas_call(
         kernel,
-        in_specs=[vmem, vmem] + [ANY] * len(after),
+        in_specs=[vmem, vmem],
         out_specs=vmem,
         out_shape=jax.ShapeDtypeStruct((1, train.shape[0]), jnp.bfloat16),
         name="add_norm",
-    )(train[None, :], step[None, :], *after)
+    )(train[None, :], step[None, :])
 
 
 def collect_norm(pieces, rows, n, width):
@@ -160,8 +161,8 @@
     def swap(x, axis, size, mask):
         return lax.ppermute(x, axis, [(i, i ^ mask) for i in range(size)])
 
-    def gather_norm(after):
-        norm = add_norm(norm_train, norm_step, after)
+    def gather_norm():
+        norm = add_norm(norm_train, norm_step)
         mine = lax.axis_index("tp")
         bit = 1
         while bit < t:
@@ -175,14 +176,12 @@
             bit *= 2
         return norm
 
-    dummy = jnp.zeros((1, width), jnp.bfloat16)
     norm_pair = max(len(pairs) - 2, 0)
     carrier = pairs[norm_pair][-1]
     held = {}
     for index in range(pieces):
-        extra = 16 if index == carrier else 0
-        norm = gather_norm([]) if extra else dummy
-        held[index] = {0: merge_piece(train_up, low_up, high_up, norm, index, rows, extra, [])}
+        norm = gather_norm() if index == carrier else None
+        held[index] = {0: merge_piece(train_up, low_up, high_up, norm, index, rows)}
 
     early, late = [], []
     for pair in pairs:

time: 291 us -> 291 us (level)
  no operation moved by 1% of the time
where the time goes in v2:
time: 291 us; the launch traced here: 290 us
  waiting for transfers between devices  179 us (62%)
  Pallas kernels  65.1 us (22%)
  starting transfers between devices  39.1 us (13%)
  other arithmetic  3.68 us (1%)
    ppermute x58, waiting for transfers between devices, swap(): return lax.ppermute(x, axis, [(i, i ^ mask) for i in range(size)])  179 us
    pallas_call x8, Pallas kernels, place(): pl.pallas_call(functools.partial(place_kernel, count=count, slots=tuple(s...  42.1 us
    ppermute x58, starting transfers between devices, swap(): return lax.ppermute(x, axis, [(i, i ^ mask) for i in range(size)])  39.1 us
    pallas_call x8, Pallas kernels, merge_piece(): pl.pallas_call(functools.partial(merge_kernel, tile=128), grid=(1,), in_s...  20.3 us
  transfers between devices with their start and end apart: 58, of which 27 were waited for; matrix products, arithmetic and copies ran while one was open for 1% of the time, Pallas kernels for 21%

profile of v2, /device:TPU:0, one launch (start us, length us, event | category | flops | bytes accessed | tf_op | source)
XLA Modules:
  0.0 290.0 jit_solution(3213152081916843525)
XLA Ops:
  0.6 2.5 shard_map.74.refs_0_
  3.1 3.0 %collective-permute-start.20 = (bf16[640,640]{1,0:T(8,128)(2,1)}, bf16[640,640]{1,0:T(8,128)(2,1)S(1)}, u32[]{:S(2)}, u32[]{:S(2)}) collective-permute-start(bf16[640,640]{1,0:T(8,128)(2,1)} %shard_map.74.refs_0_), channel_id=1, source_target_pairs={{0,8},{4,12},{8,0},{12,4},{16,24},{20,28},{24,16},{28,20},{1,9},{5... | collective-permute-start | bytes 2457608 | tf_op jit(solution)/shard_map/ppermute | solution.py:162
  6.1 1.5 collective-permute-start.50
  7.6 2.5 shard_map.75.refs_3_
  11.9 2.1 collective-permute-start.8
  14.0 1.8 collective-permute-done.8
  16.6 3.0 %collective-permute-start.9 = (bf16[1,320]{1,0:T(2,128)(2,1)S(1)}, bf16[1,320]{1,0:T(2,128)(2,1)S(1)}, u32[]{:S(2)}, u32[]{:S(2)}) collective-permute-start(bf16[1,320]{1,0:T(2,128)(2,1)S(1)} %broadcast_select_fusion.1), channel_id=1, source_target_pairs={{0,2},{1,3},{2,0},{3,1},{4,6},{5,7},{6,4},{7,5},{8,10},{9,11},{10,... | collective-permute-start | bytes 1928 | tf_op jit(solution)/shard_map/ppermute | solution.py:162
  19.6 1.6 collective-permute-done.9
  21.2 4.2 %collective-permute-done.20.refs_1_ = bf16[640,640]{1,0:T(8,128)(2,1)S(1)} collective-permute-done((bf16[640,640]{1,0:T(8,128)(2,1)}, bf16[640,640]{1,0:T(8,128)(2,1)S(1)}, u32[]{:S(2)}, u32[]{:S(2)}) %collective-permute-start.20) | collective-permute-done | bytes 819232 | tf_op jit(solution)/shard_map/ppermute | solution.py:162
  25.4 2.8 shard_map.72.refs_0_
  28.2 15.4 %collective-permute-done.22.refs_4_ = bf16[640,640]{1,0:T(8,128)(2,1)S(1)} collective-permute-done((bf16[640,640]{1,0:T(8,128)(2,1)}, bf16[640,640]{1,0:T(8,128)(2,1)S(1)}, u32[]{:S(2)}, u32[]{:S(2)}) %collective-permute-start.22) | collective-permute-done | bytes 819232 | tf_op jit(solution)/shard_map/ppermute | solution.py:162
  43.9 2.5 shard_map.73.refs_3_
  46.4 1.7 collective-permute-start.16
  48.4 1.7 collective-permute-start.43
  50.1 14.9 %collective-permute-done.14.refs_1_ = bf16[640,640]{1,0:T(8,128)(2,1)} collective-permute-done((bf16[640,640]{1,0:T(8,128)(2,1)}, bf16[640,640]{1,0:T(8,128)(2,1)}, u32[]{:S(2)}, u32[]{:S(2)}) %collective-permute-start.14) | collective-permute-done | bytes 819232 | tf_op jit(solution)/shard_map/ppermute | solution.py:162
  65.0 2.5 shard_map.70.refs_0_
  67.8 1.7 collective-permute-start.6
  69.5 13.6 %collective-permute-done.42.refs_2_ = bf16[640,640]{1,0:T(8,128)(2,1)} collective-permute-done((bf16[640,640]{1,0:T(8,128)(2,1)}, bf16[640,640]{1,0:T(8,128)(2,1)}, u32[]{:S(2)}, u32[]{:S(2)}) %collective-permute-start.42) | collective-permute-done | bytes 819232 | tf_op jit(solution)/shard_map/ppermute | solution.py:162
  83.1 1.5 collective-permute-start.34
  84.6 2.5 shard_map.68.refs_0_
  87.2 1.5 collective-permute-start
  88.7 2.5 shard_map.69.refs_3_
  91.7 8.4 %collective-permute-done.6.refs_1_ = bf16[640,640]{1,0:T(8,128)(2,1)} collective-permute-done((bf16[640,640]{1,0:T(8,128)(2,1)}, bf16[640,640]{1,0:T(8,128)(2,1)}, u32[]{:S(2)}, u32[]{:S(2)}) %collective-permute-start.6) | collective-permute-done | bytes 819232 | tf_op jit(solution)/shard_map/ppermute | solution.py:162
  100.1 1.5 collective-permute-start.26
  101.6 2.8 collective-permute-done.34.refs_2_
  104.4 1.4 collective-permute-start.27
  105.9 11.8 %collective-permute-done.refs_1_ = bf16[640,640]{1,0:T(8,128)(2,1)} collective-permute-done((bf16[640,640]{1,0:T(8,128)(2,1)}, bf16[640,640]{1,0:T(8,128)(2,1)}, u32[]{:S(2)}, u32[]{:S(2)}) %collective-permute-start) | collective-permute-done | bytes 819232 | tf_op jit(solution)/shard_map/ppermute | solution.py:162
  119.1 2.5 shard_map.71.refs_3_.refs_0_
  122.1 1.5 collective-permute-start.10
  123.6 16.1 %collective-permute-done.26.refs_2_ = bf16[640,640]{1,0:T(8,128)(2,1)} collective-permute-done((bf16[640,640]{1,0:T(8,128)(2,1)}, bf16[640,640]{1,0:T(8,128)(2,1)}, u32[]{:S(2)}, u32[]{:S(2)}) %collective-permute-start.26) | collective-permute-done | bytes 819232 | tf_op jit(solution)/shard_map/ppermute | solution.py:162
  139.7 1.4 collective-permute-start.35
  141.7 12.8 %collective-permute-done.10.refs_4_ = bf16[656,640]{1,0:T(8,128)(2,1)S(1)} collective-permute-done((bf16[656,640]{1,0:T(8,128)(2,1)}, bf16[656,640]{1,0:T(8,128)(2,1)S(1)}, u32[]{:S(2)}, u32[]{:S(2)}) %collective-permute-start.10) | collective-permute-done | bytes 839712 | tf_op jit(solution)/shard_map/ppermute | solution.py:162
  155.5 1.4 collective-permute-done.54.refs_8_
  166.4 1.5 collective-permute-start.23
  171.3 15.2 %collective-permute-done.21.refs_0_ = bf16[640,640]{1,0:T(8,128)(2,1)S(1)} collective-permute-done((bf16[640,640]{1,0:T(8,128)(2,1)}, bf16[640,640]{1,0:T(8,128)(2,1)S(1)}, u32[]{:S(2)}, u32[]{:S(2)}) %collective-permute-start.21) | collective-permute-done | bytes 819232 | tf_op jit(solution)/shard_map/ppermute | solution.py:162
  188.9 15.1 %collective-permute-done.15.refs_0_ = bf16[640,640]{1,0:T(8,128)(2,1)S(1)} collective-permute-done((bf16[640,640]{1,0:T(8,128)(2,1)}, bf16[640,640]{1,0:T(8,128)(2,1)S(1)}, u32[]{:S(2)}, u32[]{:S(2)}) %collective-permute-start.15) | collective-permute-done | bytes 819232 | tf_op jit(solution)/shard_map/ppermute | solution.py:162
  206.1 15.6 %collective-permute-done.7.refs_0_ = bf16[640,640]{1,0:T(8,128)(2,1)} collective-permute-done((bf16[640,640]{1,0:T(8,128)(2,1)}, bf16[640,640]{1,0:T(8,128)(2,1)}, u32[]{:S(2)}, u32[]{:S(2)}) %collective-permute-start.7) | collective-permute-done | bytes 819232 | tf_op jit(solution)/shard_map/ppermute | solution.py:162
  221.7 16.7 %collective-permute-done.1.refs_0_ = bf16[640,640]{1,0:T(8,128)(2,1)} collective-permute-done((bf16[640,640]{1,0:T(8,128)(2,1)}, bf16[640,640]{1,0:T(8,128)(2,1)}, u32[]{:S(2)}, u32[]{:S(2)}) %collective-permute-start.1) | collective-permute-done | bytes 819232 | tf_op jit(solution)/shard_map/ppermute | solution.py:162
  239.1 2.0 collective-permute-done.11.refs_1_.refs_6_
  244.9 7.6 %shard_map.76.refs_12_ = bf16[5120,5120]{1,0:T(8,128)(2,1)} custom-call(bf16[640,640]{1,0:T(8,128)(2,1)} %shard_map.74.refs_0_, bf16[640,640]{1,0:T(8,128)(2,1)} %copy-done.15, bf16[640,640]{1,0:T(8,128)(2,1)} %copy-done.16, bf16[640,640]{1,0:T(8,128)(2,1)} %shard_map.75.refs_3_, bf16[640,640]{1,0:T(8,128)(2,1)} %copy-done.17, bf16[640,640]{1,0:T(8,128)(2,1)} %copy-done.18, ...), custom_call_target="tpu_custom_call" | custom-call | bytes 19660800 | tf_op jit(solution)/shard_map/pallas_call | solution.py:94
  252.5 7.6 %shard_map.77.refs_12_ = bf16[5120,5120]{1,0:T(8,128)(2,1)} custom-call(bf16[640,640]{1,0:T(8,128)(2,1)} %shard_map.72.refs_0_, bf16[640,640]{1,0:T(8,128)(2,1)} %collective-permute-done.14.refs_1_, bf16[640,640]{1,0:T(8,128)(2,1)} %collective-permute-done.42.refs_2_, bf16[640,640]{1,0:T(8,128)(2,1)} %shard_map.73.refs_3_, ...), custom_call_target="tpu_custom_call", output_to_operand_aliasing={{}: (12, {})} | custom-call | bytes 19660800 | tf_op jit(solution)/shard_map/pallas_call | solution.py:94
  260.1 7.6 %shard_map.78.refs_12_ = bf16[5120,5120]{1,0:T(8,128)(2,1)} custom-call(bf16[640,640]{1,0:T(8,128)(2,1)} %shard_map.70.refs_0_, bf16[640,640]{1,0:T(8,128)(2,1)} %collective-permute-done.6.refs_1_, bf16[640,640]{1,0:T(8,128)(2,1)} %copy-done.5, bf16[656,640]{1,0:T(8,128)(2,1)} %shard_map.71.refs_3_.refs_0_, ...), custom_call_target="tpu_custom_call", output_to_operand_aliasing={{}: (12, {})} | custom-call | bytes 19660800 | tf_op jit(solution)/shard_map/pallas_call | solution.py:94
  267.7 7.6 %shard_map.79.refs_4_ = bf16[5120,5120]{1,0:T(8,128)(2,1)} custom-call(bf16[640,640]{1,0:T(8,128)(2,1)} %shard_map.68.refs_0_, bf16[640,640]{1,0:T(8,128)(2,1)} %collective-permute-done.refs_1_, bf16[640,640]{1,0:T(8,128)(2,1)} %collective-permute-done.26.refs_2_, bf16[640,640]{1,0:T(8,128)(2,1)} %shard_map.69.refs_3_, ...), custom_call_target="tpu_custom_call", output_to_operand_aliasing={{}: (12, {})} | custom-call | bytes 19660800 | tf_op jit(solution)/shard_map/pallas_call | solution.py:94
  275.3 2.9 %shard_map.80.refs_4_ = bf16[5120,5120]{1,0:T(8,128)(2,1)} custom-call(bf16[640,640]{1,0:T(8,128)(2,1)} %copy-done.9, bf16[640,640]{1,0:T(8,128)(2,1)} %copy-done.11, bf16[640,640]{1,0:T(8,128)(2,1)} %copy-done.12, bf16[640,640]{1,0:T(8,128)(2,1)} %copy-done.14, bf16[5120,5120]{1,0:T(8,128)(2,1)} %shard_map.79.refs_4_), custom_call_target="tpu_custom_call", output_to_operand_aliasing={{}: (4, {})} | custom-call | bytes 6553600 | tf_op jit(solution)/shard_map/pallas_call | solution.py:94
  278.3 2.9 %shard_map.81.refs_4_ = bf16[5120,5120]{1,0:T(8,128)(2,1)} custom-call(bf16[640,640]{1,0:T(8,128)(2,1)} %copy-done.10, bf16[640,640]{1,0:T(8,128)(2,1)} %collective-permute-done.17.refs_1_, bf16[640,640]{1,0:T(8,128)(2,1)} %copy-done.13, bf16[640,640]{1,0:T(8,128)(2,1)} %collective-permute-done.19.refs_3_, ...), custom_call_target="tpu_custom_call", output_to_operand_aliasing={{}: (4, {})} | custom-call | bytes 6553600 | tf_op jit(solution)/shard_map/pallas_call | solution.py:94
  281.2 1.5 collect_norm.1
  284.1 2.9 %shard_map.82.refs_4_ = bf16[5120,5120]{1,0:T(8,128)(2,1)} custom-call(bf16[640,640]{1,0:T(8,128)(2,1)} %collective-permute-done.7.refs_0_, bf16[656,640]{1,0:T(8,128)(2,1)} %collective-permute-done.11.refs_1_.refs_6_, bf16[640,640]{1,0:T(8,128)(2,1)} %collective-permute-done.12.refs_2_, ...), custom_call_target="tpu_custom_call", output_to_operand_aliasing={{}: (4, {})} | custom-call | bytes 6553600 | tf_op jit(solution)/shard_map/pallas_call | solution.py:94
  287.1 2.9 %shard_map.83 = bf16[5120,5120]{1,0:T(8,128)(2,1)} custom-call(bf16[640,640]{1,0:T(8,128)(2,1)} %collective-permute-done.1.refs_0_, bf16[640,640]{1,0:T(8,128)(2,1)} %collective-permute-done.3.refs_1_, bf16[640,640]{1,0:T(8,128)(2,1)} %collective-permute-done.4.refs_2_, ...), custom_call_target="tpu_custom_call", output_to_operand_aliasing={{}: (4, {})} | custom-call | bytes 6553600 | tf_op jit(solution)/shard_map/pallas_call | solution.py:94
  (155 shorter events, 31.0 us)
Async XLA Ops:
  3.1 22.3 %collective-permute-start.20 = (bf16[640,640]{1,0:T(8,128)(2,1)}, bf16[640,640]{1,0:T(8,128)(2,1)S(1)}, u32[]{:S(2)}, u32[]{:S(2)}) collective-permute-start(bf16[640,640]{1,0:T(8,128)(2,1)} %shard_map.74.refs_0_), channel_id=1, source_target_pairs={{0,8},{4,12},{8,0},{12,4},{16,24},{20,28},{24,16},{28,20},{1,9},{5... | collective-permute-start | bytes 2457608 | tf_op jit(solution)/shard_map/ppermute | solution.py:162
  6.1 40.3 %collective-permute-start.50 = (bf16[640,640]{1,0:T(8,128)(2,1)}, bf16[640,640]{1,0:T(8,128)(2,1)S(1)}, u32[]{:S(2)}, u32[]{:S(2)}) collective-permute-start(bf16[640,640]{1,0:T(8,128)(2,1)} %shard_map.74.refs_0_), channel_id=1, source_target_pairs={{0,16},{4,20},{8,24},{12,28},{16,0},{20,4},{24,8},{28,12},{1,17},{... | collective-permute-start | bytes 2457608 | tf_op jit(solution)/shard_map/ppermute | solution.py:162
  10.1 33.5 %collective-permute-start.22 = (bf16[640,640]{1,0:T(8,128)(2,1)}, bf16[640,640]{1,0:T(8,128)(2,1)S(1)}, u32[]{:S(2)}, u32[]{:S(2)}) collective-permute-start(bf16[640,640]{1,0:T(8,128)(2,1)} %shard_map.75.refs_3_), channel_id=1, source_target_pairs={{0,16},{4,20},{8,24},{12,28},{16,0},{20,4},{24,8},{28,12},{1,17},{... | collective-permute-start | bytes 2457608 | tf_op jit(solution)/shard_map/ppermute | solution.py:162
  10.6 37.5 %collective-permute-start.51 = (bf16[640,640]{1,0:T(8,128)(2,1)}, bf16[640,640]{1,0:T(8,128)(2,1)S(1)}, u32[]{:S(2)}, u32[]{:S(2)}) collective-permute-start(bf16[640,640]{1,0:T(8,128)(2,1)} %shard_map.75.refs_3_), channel_id=1, source_target_pairs={{0,8},{4,12},{8,0},{12,4},{16,24},{20,28},{24,16},{28,20},{1,9},{5... | collective-permute-start | bytes 2457608 | tf_op jit(solution)/shard_map/ppermute | solution.py:162
  21.2 27.3 %collective-permute-start.52 = (bf16[640,640]{1,0:T(8,128)(2,1)}, bf16[640,640]{1,0:T(8,128)(2,1)}, u32[]{:S(2)}, u32[]{:S(2)}) collective-permute-start(bf16[640,640]{1,0:T(8,128)(2,1)} %shard_map.74.refs_0_), channel_id=1, source_target_pairs={{0,4},{4,0},{8,12},{12,8},{16,20},{20,16},{24,28},{28,24},{1,5},{5... | collective-permute-start | bytes 2457608 | tf_op jit(solution)/shard_map/ppermute | solution.py:162
  25.4 24.7 %collective-permute-start.55 = (bf16[640,640]{1,0:T(8,128)(2,1)}, bf16[640,640]{1,0:T(8,128)(2,1)}, u32[]{:S(2)}, u32[]{:S(2)}) collective-permute-start(bf16[640,640]{1,0:T(8,128)(2,1)} %shard_map.75.refs_3_), channel_id=1, source_target_pairs={{0,4},{4,0},{8,12},{12,8},{16,20},{20,16},{24,28},{28,24},{1,5},{5... | collective-permute-start | bytes 2457608 | tf_op jit(solution)/shard_map/ppermute | solution.py:162
  43.5 21.4 %collective-permute-start.14 = (bf16[640,640]{1,0:T(8,128)(2,1)}, bf16[640,640]{1,0:T(8,128)(2,1)}, u32[]{:S(2)}, u32[]{:S(2)}) collective-permute-start(bf16[640,640]{1,0:T(8,128)(2,1)} %shard_map.72.refs_0_), channel_id=1, source_target_pairs={{0,8},{4,12},{8,0},{12,4},{16,24},{20,28},{24,16},{28,20},{1,9},{5... | collective-permute-start | bytes 2457608 | tf_op jit(solution)/shard_map/ppermute | solution.py:162
  46.4 21.4 %collective-permute-start.16 = (bf16[640,640]{1,0:T(8,128)(2,1)}, bf16[640,640]{1,0:T(8,128)(2,1)}, u32[]{:S(2)}, u32[]{:S(2)}) collective-permute-start(bf16[640,640]{1,0:T(8,128)(2,1)} %shard_map.73.refs_3_), channel_id=1, source_target_pairs={{0,16},{4,20},{8,24},{12,28},{16,0},{20,4},{24,8},{28,12},{1,17},{... | collective-permute-start | bytes 2457608 | tf_op jit(solution)/shard_map/ppermute | solution.py:162
  48.1 35.0 %collective-permute-start.42 = (bf16[640,640]{1,0:T(8,128)(2,1)}, bf16[640,640]{1,0:T(8,128)(2,1)}, u32[]{:S(2)}, u32[]{:S(2)}) collective-permute-start(bf16[640,640]{1,0:T(8,128)(2,1)} %shard_map.72.refs_0_), channel_id=1, source_target_pairs={{0,16},{4,20},{8,24},{12,28},{16,0},{20,4},{24,8},{28,12},{1,17},{... | collective-permute-start | bytes 2457608 | tf_op jit(solution)/shard_map/ppermute | solution.py:162
  48.4 38.7 %collective-permute-start.43 = (bf16[640,640]{1,0:T(8,128)(2,1)}, bf16[640,640]{1,0:T(8,128)(2,1)}, u32[]{:S(2)}, u32[]{:S(2)}) collective-permute-start(bf16[640,640]{1,0:T(8,128)(2,1)} %shard_map.73.refs_3_), channel_id=1, source_target_pairs={{0,8},{4,12},{8,0},{12,4},{16,24},{20,28},{24,16},{28,20},{1,9},{5... | collective-permute-start | bytes 2457608 | tf_op jit(solution)/shard_map/ppermute | solution.py:162
  50.1 37.0 %collective-permute-start.44 = (bf16[640,640]{1,0:T(8,128)(2,1)}, bf16[640,640]{1,0:T(8,128)(2,1)}, u32[]{:S(2)}, u32[]{:S(2)}) collective-permute-start(bf16[640,640]{1,0:T(8,128)(2,1)} %shard_map.72.refs_0_), channel_id=1, source_target_pairs={{0,4},{4,0},{8,12},{12,8},{16,20},{20,16},{24,28},{28,24},{1,5},{5... | collective-permute-start | bytes 2457608 | tf_op jit(solution)/shard_map/ppermute | solution.py:162
  65.0 26.2 %collective-permute-start.47 = (bf16[640,640]{1,0:T(8,128)(2,1)}, bf16[640,640]{1,0:T(8,128)(2,1)}, u32[]{:S(2)}, u32[]{:S(2)}) collective-permute-start(bf16[640,640]{1,0:T(8,128)(2,1)} %shard_map.73.refs_3_), channel_id=1, source_target_pairs={{0,4},{4,0},{8,12},{12,8},{16,20},{20,16},{24,28},{28,24},{1,5},{5... | collective-permute-start | bytes 2457608 | tf_op jit(solution)/shard_map/ppermute | solution.py:162
  67.8 32.3 %collective-permute-start.6 = (bf16[640,640]{1,0:T(8,128)(2,1)}, bf16[640,640]{1,0:T(8,128)(2,1)}, u32[]{:S(2)}, u32[]{:S(2)}) collective-permute-start(bf16[640,640]{1,0:T(8,128)(2,1)} %shard_map.70.refs_0_), channel_id=1, source_target_pairs={{0,8},{4,12},{8,0},{12,4},{16,24},{20,28},{24,16},{28,20},{1,9},{5... | collective-permute-start | bytes 2457608 | tf_op jit(solution)/shard_map/ppermute | solution.py:162
  83.1 21.3 %collective-permute-start.34 = (bf16[640,640]{1,0:T(8,128)(2,1)}, bf16[640,640]{1,0:T(8,128)(2,1)S(1)}, u32[]{:S(2)}, u32[]{:S(2)}) collective-permute-start(bf16[640,640]{1,0:T(8,128)(2,1)} %shard_map.70.refs_0_), channel_id=1, source_target_pairs={{0,16},{4,20},{8,24},{12,28},{16,0},{20,4},{24,8},{28,12},{1,17},{... | collective-permute-start | bytes 2457608 | tf_op jit(solution)/shard_map/ppermute | solution.py:162
  87.1 18.7 %collective-permute-start.36 = (bf16[640,640]{1,0:T(8,128)(2,1)}, bf16[640,640]{1,0:T(8,128)(2,1)S(1)}, u32[]{:S(2)}, u32[]{:S(2)}) collective-permute-start(bf16[640,640]{1,0:T(8,128)(2,1)} %shard_map.70.refs_0_), channel_id=1, source_target_pairs={{0,4},{4,0},{8,12},{12,8},{16,20},{20,16},{24,28},{28,24},{1,5},{5... | collective-permute-start | bytes 2457608 | tf_op jit(solution)/shard_map/ppermute | solution.py:162
  87.2 30.5 %collective-permute-start = (bf16[640,640]{1,0:T(8,128)(2,1)}, bf16[640,640]{1,0:T(8,128)(2,1)}, u32[]{:S(2)}, u32[]{:S(2)}) collective-permute-start(bf16[640,640]{1,0:T(8,128)(2,1)} %shard_map.68.refs_0_), channel_id=1, source_target_pairs={{0,8},{4,12},{8,0},{12,4},{16,24},{20,28},{24,16},{28,20},{1,9},{5... | collective-permute-start | bytes 2457608 | tf_op jit(solution)/shard_map/ppermute | solution.py:162
  91.2 30.9 %collective-permute-start.2 = (bf16[640,640]{1,0:T(8,128)(2,1)}, bf16[640,640]{1,0:T(8,128)(2,1)}, u32[]{:S(2)}, u32[]{:S(2)}) collective-permute-start(bf16[640,640]{1,0:T(8,128)(2,1)} %shard_map.69.refs_3_), channel_id=1, source_target_pairs={{0,16},{4,20},{8,24},{12,28},{16,0},{20,4},{24,8},{28,12},{1,17},{... | collective-permute-start | bytes 2457608 | tf_op jit(solution)/shard_map/ppermute | solution.py:162
  100.1 39.6 %collective-permute-start.26 = (bf16[640,640]{1,0:T(8,128)(2,1)}, bf16[640,640]{1,0:T(8,128)(2,1)}, u32[]{:S(2)}, u32[]{:S(2)}) collective-permute-start(bf16[640,640]{1,0:T(8,128)(2,1)} %shard_map.68.refs_0_), channel_id=1, source_target_pairs={{0,16},{4,20},{8,24},{12,28},{16,0},{20,4},{24,8},{28,12},{1,17},{... | collective-permute-start | bytes 2457608 | tf_op jit(solution)/shard_map/ppermute | solution.py:162
  104.4 36.6 %collective-permute-start.27 = (bf16[640,640]{1,0:T(8,128)(2,1)}, bf16[640,640]{1,0:T(8,128)(2,1)}, u32[]{:S(2)}, u32[]{:S(2)}) collective-permute-start(bf16[640,640]{1,0:T(8,128)(2,1)} %shard_map.69.refs_3_), channel_id=1, source_target_pairs={{0,8},{4,12},{8,0},{12,4},{16,24},{20,28},{24,16},{28,20},{1,9},{5... | collective-permute-start | bytes 2457608 | tf_op jit(solution)/shard_map/ppermute | solution.py:162
  105.9 35.2 %collective-permute-start.28 = (bf16[640,640]{1,0:T(8,128)(2,1)}, bf16[640,640]{1,0:T(8,128)(2,1)}, u32[]{:S(2)}, u32[]{:S(2)}) collective-permute-start(bf16[640,640]{1,0:T(8,128)(2,1)} %shard_map.68.refs_0_), channel_id=1, source_target_pairs={{0,4},{4,0},{8,12},{12,8},{16,20},{20,16},{24,28},{28,24},{1,5},{5... | collective-permute-start | bytes 2457608 | tf_op jit(solution)/shard_map/ppermute | solution.py:162
  117.6 23.9 %collective-permute-start.31 = (bf16[640,640]{1,0:T(8,128)(2,1)}, bf16[640,640]{1,0:T(8,128)(2,1)}, u32[]{:S(2)}, u32[]{:S(2)}) collective-permute-start(bf16[640,640]{1,0:T(8,128)(2,1)} %shard_map.69.refs_3_), channel_id=1, source_target_pairs={{0,4},{4,0},{8,12},{12,8},{16,20},{20,16},{24,28},{28,24},{1,5},{5... | collective-permute-start | bytes 2457608 | tf_op jit(solution)/shard_map/ppermute | solution.py:162
  122.1 32.3 %collective-permute-start.10 = (bf16[656,640]{1,0:T(8,128)(2,1)}, bf16[656,640]{1,0:T(8,128)(2,1)S(1)}, u32[]{:S(2)}, u32[]{:S(2)}) collective-permute-start(bf16[656,640]{1,0:T(8,128)(2,1)} %shard_map.71.refs_3_.refs_0_), channel_id=1, source_target_pairs={{0,16},{4,20},{8,24},{12,28},{16,0},{20,4},{24,8},{28,12},{1,17},{... | collective-permute-start | bytes 2519048 | tf_op jit(solution)/shard_map/ppermute | solution.py:162
  139.7 14.8 %collective-permute-start.35 = (bf16[656,640]{1,0:T(8,128)(2,1)}, bf16[656,640]{1,0:T(8,128)(2,1)S(1)}, u32[]{:S(2)}, u32[]{:S(2)}) collective-permute-start(bf16[656,640]{1,0:T(8,128)(2,1)} %shard_map.71.refs_3_.refs_0_), channel_id=1, source_target_pairs={{0,8},{4,12},{8,0},{12,4},{16,24},{20,28},{24,16},{28,20},{1,9},{5... | collective-permute-start | bytes 2519048 | tf_op jit(solution)/shard_map/ppermute | solution.py:162
  141.1 13.9 %collective-permute-start.39 = (bf16[656,640]{1,0:T(8,128)(2,1)}, bf16[656,640]{1,0:T(8,128)(2,1)S(1)}, u32[]{:S(2)}, u32[]{:S(2)}) collective-permute-start(bf16[656,640]{1,0:T(8,128)(2,1)} %shard_map.71.refs_3_.refs_0_), channel_id=1, source_target_pairs={{0,4},{4,0},{8,12},{12,8},{16,20},{20,16},{24,28},{28,24},{1,5},{5... | collective-permute-start | bytes 2519048 | tf_op jit(solution)/shard_map/ppermute | solution.py:162
  141.1 14.0 %collective-permute-start.53 = (bf16[640,640]{1,0:T(8,128)(2,1)}, bf16[640,640]{1,0:T(8,128)(2,1)S(1)}, u32[]{:S(2)}, u32[]{:S(2)}) collective-permute-start(bf16[640,640]{1,0:T(8,128)(2,1)} %copy-done.15), channel_id=1, source_target_pairs={{0,4},{4,0},{8,12},{12,8},{16,20},{20,16},{24,28},{28,24},{1,5},{5... | collective-permute-start | bytes 2457608 | tf_op jit(solution)/shard_map/ppermute | solution.py:162
  141.6 13.9 %collective-permute-start.56 = (bf16[640,640]{1,0:T(8,128)(2,1)}, bf16[640,640]{1,0:T(8,128)(2,1)S(1)}, u32[]{:S(2)}, u32[]{:S(2)}) collective-permute-start(bf16[640,640]{1,0:T(8,128)(2,1)} %copy-done.17), channel_id=1, source_target_pairs={{0,4},{4,0},{8,12},{12,8},{16,20},{20,16},{24,28},{28,24},{1,5},{5... | collective-permute-start | bytes 2457608 | tf_op jit(solution)/shard_map/ppermute | solution.py:162
  155.5 6.2 %collective-permute-start.46 = (bf16[640,640]{1,0:T(8,128)(2,1)}, bf16[640,640]{1,0:T(8,128)(2,1)S(1)}, u32[]{:S(2)}, u32[]{:S(2)}) collective-permute-start(bf16[640,640]{1,0:T(8,128)(2,1)} %collective-permute-done.42.refs_2_), channel_id=1, source_target_pairs={{0,4},{4,0},{8,12},{12,8},{16,20},{20,16},{24,28},{28,24},{1,5},{5... | collective-permute-start | bytes 2457608 | tf_op jit(solution)/shard_map/ppermute | solution.py:162
  157.0 5.9 %collective-permute-start.49 = (bf16[640,640]{1,0:T(8,128)(2,1)}, bf16[640,640]{1,0:T(8,128)(2,1)S(1)}, u32[]{:S(2)}, u32[]{:S(2)}) collective-permute-start(bf16[640,640]{1,0:T(8,128)(2,1)} %collective-permute-done.43.refs_5_), channel_id=1, source_target_pairs={{0,4},{4,0},{8,12},{12,8},{16,20},{20,16},{24,28},{28,24},{1,5},{5... | collective-permute-start | bytes 2457608 | tf_op jit(solution)/shard_map/ppermute | solution.py:162
  158.1 5.9 %collective-permute-start.37 = (bf16[640,640]{1,0:T(8,128)(2,1)}, bf16[640,640]{1,0:T(8,128)(2,1)S(1)}, u32[]{:S(2)}, u32[]{:S(2)}) collective-permute-start(bf16[640,640]{1,0:T(8,128)(2,1)} %collective-permute-done.6.refs_1_), channel_id=1, source_target_pairs={{0,4},{4,0},{8,12},{12,8},{16,20},{20,16},{24,28},{28,24},{1,5},{5... | collective-permute-start | bytes 2457608 | tf_op jit(solution)/shard_map/ppermute | solution.py:162
  160.5 5.9 %collective-permute-start.29 = (bf16[640,640]{1,0:T(8,128)(2,1)}, bf16[640,640]{1,0:T(8,128)(2,1)S(1)}, u32[]{:S(2)}, u32[]{:S(2)}) collective-permute-start(bf16[640,640]{1,0:T(8,128)(2,1)} %collective-permute-done.refs_1_), channel_id=1, source_target_pairs={{0,4},{4,0},{8,12},{12,8},{16,20},{20,16},{24,28},{28,24},{1,5},{5... | collective-permute-start | bytes 2457608 | tf_op jit(solution)/shard_map/ppermute | solution.py:162
  161.6 6.2 %collective-permute-start.32 = (bf16[640,640]{1,0:T(8,128)(2,1)}, bf16[640,640]{1,0:T(8,128)(2,1)S(1)}, u32[]{:S(2)}, u32[]{:S(2)}) collective-permute-start(bf16[640,640]{1,0:T(8,128)(2,1)} %collective-permute-done.2.refs_4_), channel_id=1, source_target_pairs={{0,4},{4,0},{8,12},{12,8},{16,20},{20,16},{24,28},{28,24},{1,5},{5... | collective-permute-start | bytes 2457608 | tf_op jit(solution)/shard_map/ppermute | solution.py:162
  162.8 6.2 %collective-permute-start.30 = (bf16[640,640]{1,0:T(8,128)(2,1)}, bf16[640,640]{1,0:T(8,128)(2,1)S(1)}, u32[]{:S(2)}, u32[]{:S(2)}) collective-permute-start(bf16[640,640]{1,0:T(8,128)(2,1)} %collective-permute-done.26.refs_2_), channel_id=1, source_target_pairs={{0,4},{4,0},{8,12},{12,8},{16,20},{20,16},{24,28},{28,24},{1,5},{5... | collective-permute-start | bytes 2457608 | tf_op jit(solution)/shard_map/ppermute | solution.py:162
  164.0 6.2 %collective-permute-start.33 = (bf16[640,640]{1,0:T(8,128)(2,1)}, bf16[640,640]{1,0:T(8,128)(2,1)S(1)}, u32[]{:S(2)}, u32[]{:S(2)}) collective-permute-start(bf16[640,640]{1,0:T(8,128)(2,1)} %collective-permute-done.27.refs_5_), channel_id=1, source_target_pairs={{0,4},{4,0},{8,12},{12,8},{16,20},{20,16},{24,28},{28,24},{1,5},{5... | collective-permute-start | bytes 2457608 | tf_op jit(solution)/shard_map/ppermute | solution.py:162
  165.2 21.3 %collective-permute-start.21 = (bf16[640,640]{1,0:T(8,128)(2,1)}, bf16[640,640]{1,0:T(8,128)(2,1)S(1)}, u32[]{:S(2)}, u32[]{:S(2)}) collective-permute-start(bf16[640,640]{1,0:T(8,128)(2,1)} %copy-done.15), channel_id=1, source_target_pairs={{0,16},{4,20},{8,24},{12,28},{16,0},{20,4},{24,8},{28,12},{1,17},{... | collective-permute-start | bytes 2457608 | tf_op jit(solution)/shard_map/ppermute | solution.py:162
  166.4 21.4 %collective-permute-start.23 = (bf16[640,640]{1,0:T(8,128)(2,1)}, bf16[640,640]{1,0:T(8,128)(2,1)S(1)}, u32[]{:S(2)}, u32[]{:S(2)}) collective-permute-start(bf16[640,640]{1,0:T(8,128)(2,1)} %copy-done.17), channel_id=1, source_target_pairs={{0,8},{4,12},{8,0},{12,4},{16,24},{20,28},{24,16},{28,20},{1,9},{5... | collective-permute-start | bytes 2457608 | tf_op jit(solution)/shard_map/ppermute | solution.py:162
  167.9 36.2 %collective-permute-start.15 = (bf16[640,640]{1,0:T(8,128)(2,1)}, bf16[640,640]{1,0:T(8,128)(2,1)S(1)}, u32[]{:S(2)}, u32[]{:S(2)}) collective-permute-start(bf16[640,640]{1,0:T(8,128)(2,1)} %collective-permute-done.14.refs_1_), channel_id=1, source_target_pairs={{0,16},{4,20},{8,24},{12,28},{16,0},{20,4},{24,8},{28,12},{1,17},{... | collective-permute-start | bytes 2457608 | tf_op jit(solution)/shard_map/ppermute | solution.py:162
  169.1 36.1 %collective-permute-start.17 = (bf16[640,640]{1,0:T(8,128)(2,1)}, bf16[640,640]{1,0:T(8,128)(2,1)}, u32[]{:S(2)}, u32[]{:S(2)}) collective-permute-start(bf16[640,640]{1,0:T(8,128)(2,1)} %collective-permute-done.16.refs_4_), channel_id=1, source_target_pairs={{0,8},{4,12},{8,0},{12,4},{16,24},{20,28},{24,16},{28,20},{1,9},{5... | collective-permute-start | bytes 2457608 | tf_op jit(solution)/shard_map/ppermute | solution.py:162
  170.2 51.5 %collective-permute-start.7 = (bf16[640,640]{1,0:T(8,128)(2,1)}, bf16[640,640]{1,0:T(8,128)(2,1)}, u32[]{:S(2)}, u32[]{:S(2)}) collective-permute-start(bf16[640,640]{1,0:T(8,128)(2,1)} %collective-permute-done.6.refs_1_), channel_id=1, source_target_pairs={{0,16},{4,20},{8,24},{12,28},{16,0},{20,4},{24,8},{28,12},{1,17},{... | collective-permute-start | bytes 2457608 | tf_op jit(solution)/shard_map/ppermute | solution.py:162
  186.5 52.5 %collective-permute-start.40 = (bf16[656,640]{1,0:T(8,128)(2,1)S(1)}, bf16[656,640]{1,0:T(8,128)(2,1)S(1)}, u32[]{:S(2)}, u32[]{:S(2)}) collective-permute-start(bf16[656,640]{1,0:T(8,128)(2,1)S(1)} %collective-permute-done.10.refs_4_), channel_id=1, source_target_pairs={{0,4},{4,0},{8,12},{12,8},{16,20},{20,16},{24,28},{28,24},{1,5},{5... | collective-permute-start | bytes 2519048 | tf_op jit(solution)/shard_map/ppermute | solution.py:162
  187.8 50.6 %collective-permute-start.1 = (bf16[640,640]{1,0:T(8,128)(2,1)}, bf16[640,640]{1,0:T(8,128)(2,1)}, u32[]{:S(2)}, u32[]{:S(2)}) collective-permute-start(bf16[640,640]{1,0:T(8,128)(2,1)} %collective-permute-done.refs_1_), channel_id=1, source_target_pairs={{0,16},{4,20},{8,24},{12,28},{16,0},{20,4},{24,8},{28,12},{1,17},{... | collective-permute-start | bytes 2457608 | tf_op jit(solution)/shard_map/ppermute | solution.py:162
  204.0 34.4 %collective-permute-start.3 = (bf16[640,640]{1,0:T(8,128)(2,1)}, bf16[640,640]{1,0:T(8,128)(2,1)}, u32[]{:S(2)}, u32[]{:S(2)}) collective-permute-start(bf16[640,640]{1,0:T(8,128)(2,1)} %collective-permute-done.2.refs_4_), channel_id=1, source_target_pairs={{0,8},{4,12},{8,0},{12,4},{16,24},{20,28},{24,16},{28,20},{1,9},{5... | collective-permute-start | bytes 2457608 | tf_op jit(solution)/shard_map/ppermute | solution.py:162
  205.2 35.9 %collective-permute-start.11 = (bf16[656,640]{1,0:T(8,128)(2,1)S(1)}, bf16[656,640]{1,0:T(8,128)(2,1)}, u32[]{:S(2)}, u32[]{:S(2)}) collective-permute-start(bf16[656,640]{1,0:T(8,128)(2,1)S(1)} %collective-permute-done.10.refs_4_), channel_id=1, source_target_pairs={{0,8},{4,12},{8,0},{12,4},{16,24},{20,28},{24,16},{28,20},{1,9},{5... | collective-permute-start | bytes 2519048 | tf_op jit(solution)/shard_map/ppermute | solution.py:162
  221.7 19.4 %collective-permute-start.41 = (bf16[656,640]{1,0:T(8,128)(2,1)S(1)}, bf16[656,640]{1,0:T(8,128)(2,1)S(1)}, u32[]{:S(2)}, u32[]{:S(2)}) collective-permute-start(bf16[656,640]{1,0:T(8,128)(2,1)S(1)} %collective-permute-done.35.refs_5_.refs_2_), channel_id=1, source_target_pairs={{0,4},{4,0},{8,12},{12,8},{16,20},{20,16},{24,28},{28,24},{1,5},{5... | collective-permute-start | bytes 2519048 | tf_op jit(solution)/shard_map/ppermute | solution.py:162
  241.1 40.1 %collective-permute-start.13 = (bf16[656,640]{1,0:T(8,128)(2,1)}, bf16[656,640]{1,0:T(8,128)(2,1)}, u32[]{:S(2)}, u32[]{:S(2)}) collective-permute-start(bf16[656,640]{1,0:T(8,128)(2,1)} %collective-permute-done.11.refs_1_.refs_6_), channel_id=1, source_target_pairs={{0,4},{4,0},{8,12},{12,8},{16,20},{20,16},{24,28},{28,24},{1,5},{5... | collective-permute-start | bytes 2519048 | tf_op jit(solution)/shard_map/ppermute | solution.py:162
  242.0 36.3 %collective-permute-start.19 = (bf16[640,640]{1,0:T(8,128)(2,1)}, bf16[640,640]{1,0:T(8,128)(2,1)}, u32[]{:S(2)}, u32[]{:S(2)}) collective-permute-start(bf16[640,640]{1,0:T(8,128)(2,1)} %collective-permute-done.17.refs_1_), channel_id=1, source_target_pairs={{0,4},{4,0},{8,12},{12,8},{16,20},{20,16},{24,28},{28,24},{1,5},{5... | collective-permute-start | bytes 2457608 | tf_op jit(solution)/shard_map/ppermute | solution.py:162
  242.5 41.6 %collective-permute-start.12 = (bf16[640,640]{1,0:T(8,128)(2,1)}, bf16[640,640]{1,0:T(8,128)(2,1)}, u32[]{:S(2)}, u32[]{:S(2)}) collective-permute-start(bf16[640,640]{1,0:T(8,128)(2,1)} %collective-permute-done.7.refs_0_), channel_id=1, source_target_pairs={{0,4},{4,0},{8,12},{12,8},{16,20},{20,16},{24,28},{28,24},{1,5},{5... | collective-permute-start | bytes 2457608 | tf_op jit(solution)/shard_map/ppermute | solution.py:162
  242.6 44.4 %collective-permute-start.4 = (bf16[640,640]{1,0:T(8,128)(2,1)}, bf16[640,640]{1,0:T(8,128)(2,1)}, u32[]{:S(2)}, u32[]{:S(2)}) collective-permute-start(bf16[640,640]{1,0:T(8,128)(2,1)} %collective-permute-done.1.refs_0_), channel_id=1, source_target_pairs={{0,4},{4,0},{8,12},{12,8},{16,20},{20,16},{24,28},{28,24},{1,5},{5... | collective-permute-start | bytes 2457608 | tf_op jit(solution)/shard_map/ppermute | solution.py:162
  244.6 42.5 %collective-permute-start.5 = (bf16[640,640]{1,0:T(8,128)(2,1)}, bf16[640,640]{1,0:T(8,128)(2,1)}, u32[]{:S(2)}, u32[]{:S(2)}) collective-permute-start(bf16[640,640]{1,0:T(8,128)(2,1)} %collective-permute-done.3.refs_1_), channel_id=1, source_target_pairs={{0,4},{4,0},{8,12},{12,8},{16,20},{20,16},{24,28},{28,24},{1,5},{5... | collective-permute-start | bytes 2457608 | tf_op jit(solution)/shard_map/ppermute | solution.py:162
  (41 other events, 1480.0 us)
